TPU v7x, 32 devices: a whole 2x2x4 slice. The times are simulated.
32 devices in a mesh: dp: 2 (over x), tp: 4 (over z), sp: 4 (over y, core).
Axes of the slice: x: 2, y: 2, z: 4, core: 2. Of those that a mesh axis runs over, the one named last changes fastest.
Arguments:
- hidden: bfloat16 [128, 8192], P('dp'), parts along dimension 0
- norm_scale: bfloat16 [8192], replicated
- w_qkv: bfloat16 [8192, 10240], P(None, 'tp')
- w_out: bfloat16 [8192, 8192], P('tp')
- k_cache: bfloat16 [128, 1024, 8, 128], P('dp', 'sp', 'tp'), parts along dimension 0
- v_cache: bfloat16 [128, 1024, 8, 128], P('dp', 'sp', 'tp'), parts along dimension 0
- positions: int32 [128], P('dp'), parts along dimension 0
Outputs:
- output 1: bfloat16 [128, 8192], P('dp'), parts along dimension 0
- output 2: bfloat16 [128, 1024, 8, 128], P('dp', 'sp', 'tp'), parts along dimension 0
- output 3: bfloat16 [128, 1024, 8, 128], P('dp', 'sp', 'tp'), parts along dimension 0
There are 2 independent parts. A program takes and returns all parts, laid end to end along the dimension named above; an argument that names none is the same for every part.
All inputs are finite; a program needn't handle non-finite values.
Results may differ from a plain program's by a relative error of at most 0.00672219.
Values sent between devices are 32-bit elements.
A program may use at most 1 GiB of HBM per device.

v0:
```python
import math
import jax
import jax.numpy as jnp
from jax import lax
from jax.sharding import PartitionSpec as P


def rope_apply(head_vals, positions):
    half_dim = head_vals.shape[-1] // 2
    inv_freq = jnp.exp(jnp.arange(half_dim, dtype=jnp.float32) * (-2.0 * math.log(500000.0) / head_vals.shape[-1]))
    angles = positions.astype(jnp.float32)[:, None] * inv_freq[None, :]
    cos_part = jnp.cos(angles)[:, None, None, :]
    sin_part = jnp.sin(angles)[:, None, None, :]
    first_half = head_vals[..., :half_dim]
    second_half = head_vals[..., half_dim:]
    return jnp.concatenate([first_half * cos_part - second_half * sin_part, second_half * cos_part + first_half * sin_part], axis=-1)


def layer_norm_bf16(hidden_f32, norm_scale):
    row_mean = jnp.mean(hidden_f32, axis=-1, keepdims=True)
    centered = hidden_f32 - row_mean
    row_var = jnp.mean(centered * centered, axis=-1, keepdims=True)
    return (centered * lax.rsqrt(row_var + 1e-5) * norm_scale.astype(jnp.float32)).astype(jnp.bfloat16)


def solution(mesh):
    cache_spec = P('dp', 'sp', 'tp', None)

    def local_step(hidden, norm_scale, w_qkv, w_out, k_cache, v_cache, positions):
        n_seq, seq_local, kv_local, head_dim = k_cache.shape
        q_per_kv = w_qkv.shape[1] // (kv_local * head_dim) - 2
        hidden_f32 = hidden.astype(jnp.float32)
        normed = layer_norm_bf16(hidden_f32, norm_scale)
        qkv_proj = jnp.clip(jnp.dot(normed, w_qkv, preferred_element_type=jnp.float32).astype(jnp.bfloat16), -8.0, 8.0)
        grouped = qkv_proj.reshape(n_seq, kv_local, q_per_kv + 2, head_dim)
        rotated = rope_apply(grouped[:, :, : q_per_kv + 1].astype(jnp.float32), positions).astype(jnp.bfloat16)
        queries = rotated[:, :, :q_per_kv]
        row_index = lax.axis_index('sp') * seq_local + jnp.arange(seq_local)
        new_row = (row_index[None, :] == positions[:, None])[:, :, None, None]
        k_upd = jnp.where(new_row, rotated[:, :, q_per_kv][:, None], k_cache)
        v_upd = jnp.where(new_row, grouped[:, :, q_per_kv + 1][:, None], v_cache)
        scores = jnp.einsum('bgqd,bsgd->bgqs', queries, k_upd, preferred_element_type=jnp.float32) * (head_dim ** -0.5)
        valid_mask = row_index[None, :] <= positions[:, None]
        scores = jnp.where(valid_mask[:, None, None, :], scores, -1e30)
        local_max = jnp.max(scores, axis=-1)
        weights = jnp.exp(scores - local_max[..., None])
        local_sum = jnp.sum(weights, axis=-1)
        local_out = jnp.einsum('bgqs,bsgd->bgqd', weights.astype(jnp.bfloat16), v_upd, preferred_element_type=jnp.float32)
        global_max = lax.pmax(local_max, 'sp')
        factor = jnp.exp(local_max - global_max)
        packed = jnp.concatenate([local_out * factor[..., None], (local_sum * factor)[..., None]], axis=-1)
        merged = lax.psum(packed, 'sp')
        attn_out = merged[..., :head_dim] / merged[..., head_dim:]
        attn_flat = attn_out.reshape(n_seq, kv_local * q_per_kv * head_dim).astype(jnp.bfloat16)
        head_part = jnp.dot(attn_flat, w_out, preferred_element_type=jnp.float32)
        proj_sum = lax.psum(head_part, 'tp')
        h_out = (hidden_f32 + proj_sum).astype(jnp.bfloat16)
        return h_out, k_upd, v_upd

    return jax.shard_map(
        local_step,
        mesh=mesh,
        in_specs=(P('dp', None), P(None), P(None, 'tp'), P('tp', None), cache_spec, cache_spec, P('dp')),
        out_specs=(P('dp', None), cache_spec, cache_spec),
        check_vma=False,
    )
```

profile of v0, /device:TPU:0, one launch (start us, length us, event | category | flops | bytes accessed | tf_op | source)
XLA Modules:
  0.0 232.0 jit_solution(10851741174349728732)
XLA Ops:
  7.2 0.0 all-reduce.3.cloned.1.call-start
  7.2 1.5 convert_reduce_fusion
  8.7 1.7 fusion.7
  10.4 0.7 convert_element_type.36
  11.1 17.1 %fusion.4 = bf16[64,2560]{1,0:T(8,128)(2,1)S(1)} fusion(bf16[8192,2560]{1,0:T(8,128)(2,1)} %param.9, bf16[64,8192]{1,0:T(8,128)(2,1)} %param.7, f32[8192]{0:T(1024)S(1)} %convert_element_type.36, f32[64]{0:T(128)S(1)} %add_rsqrt_fusion, f32[64]{0:T(128)S(1)} %broadcast_multiply_fusion), kind=kOutput, calls=%fused_computation.7 | convolution fusion | flops 2687303680 | bytes 43352576 | tf_op jit(solution)/shard_map/dot_general | solution.py:34
  28.2 0.2 reshape.131
  28.4 0.1 slice.37
  28.5 0.1 slice_convert_fusion
  28.7 0.1 broadcast_compare_fusion.1
  28.8 0.2 multiply_cosine_fusion
  29.0 0.5 subtract_convert_fusion
  29.5 0.2 pad_maximum_fusion.1
  29.8 25.6 %broadcast_select_fusion = (bf16[64,256,2,128]{3,2,1,0:T(2,128)(2,1)}, bf16[64,256,2,128]{3,2,1,0:T(2,128)(2,1)S(1)}) fusion(bf16[64,256,2,128]{3,2,1,0:T(2,128)(2,1)} %param.12, pred[64,256]{1,0:T(8,128)(4,1)S(1)} %get-tuple-element.10, bf16[64,2,128]{2,1,0:T(2,128)(2,1)S(1)} %copy.27, bf16[64,256,2,128]{3,2,1,0:T(2,128)(2,1)} %param.11, ...), kind=kLoop, calls=%fused_computation | loop fusion | flops 8388608 | bytes 33636352 | tf_op jit(solution)/shard_map/jit(_where)/select_n | solution.py:41
  55.4 3.4 %copy-done = bf16[64,256,2,128]{3,2,1,0:T(2,128)(2,1)} copy-done((bf16[64,256,2,128]{3,2,1,0:T(2,128)(2,1)}, bf16[64,256,2,128]{3,2,1,0:T(2,128)(2,1)S(1)}, u32[]{:S(2)}) %copy-start) | copy-done | bytes 8388632
  58.8 2.5 %fusion.35 = (f32[64,2,8]{2,1,0:T(2,128)S(1)}, f32[64,2,8,256]{3,2,1,0:T(8,128)S(1)}) fusion(bf16[64,256,2,128]{3,2,1,0:T(2,128)(2,1)S(1)} %get-tuple-element.8, bf16[64,2,9,64]{3,2,1,0:T(8,128)(2,1)S(1)} %get-tuple-element.5, bf16[64,2,9,64]{3,2,1,0:T(8,128)(2,1)S(1)} %get-tuple-element.6, pred[64,256]{1,0:T(8,128)(4,1)S(1)} %get-tuple-element.9), kind=kOutput, calls=%fused_computation.53 | convolution fusion | flops 68418560 | bytes 9752576 | tf_op jit(solution)/shard_map/bgqd,bsgd->bgqs/dot_general | solution.py:42
  61.2 13.5 %pmax.7 = f32[64,2,8]{2,1,0:T(2,128)S(1)} all-reduce(f32[64,2,8]{2,1,0:T(2,128)S(1)} %get-tuple-element.13), channel_id=1, replica_groups=mesh['dp'=2,'tp'=4,'sp'=4] {'sp'}, use_global_device_ids=true, to_apply=%region_3.4 | all-reduce | flops 1024 | bytes 8192 | tf_op jit(solution)/shard_map/pmax | solution.py:49
  74.7 0.4 fusion.24
  75.2 0.1 multiply_bitcast_fusion
  75.2 0.8 copy.30
  76.1 4.7 %fusion.17 = f32[64,2,8,128]{3,2,1,0:T(8,128)S(1)} fusion(bf16[64,256,2,128]{3,2,1,0:T(2,128)(2,1)} %get-tuple-element.7, f32[64,2,8,256]{3,2,1,0:T(8,128)S(1)} %get-tuple-element.14, f32[64,2,8]{2,1,0:T(2,128)S(1)} %get-tuple-element.13, f32[64,2,8]{2,1,0:T(2,128)S(1)} %get-tuple-element.4), kind=kOutput, calls=%fused_computation.19 | convolution fusion | flops 67764224 | bytes 9969664 | tf_op jit(solution)/shard_map/bgqs,bsgd->bgqd/dot_general | solution.py:48
  80.8 1.1 pad_maximum_fusion
  81.8 0.0 all-reduce.3.cloned.1.call-update
  81.8 0.2 all-reduce.5.cloned.1.call-start
  82.1 36.6 %all-reduce.3.cloned.1.call-done = f32[64,2,8,129]{3,2,1,0:T(8,128)} async-done(((f32[64,2,8,129]{3,2,1,0:T(8,128)}), f32[64,2,8,129]{3,2,1,0:T(8,128)}) %all-reduce.3.cloned.1.call-update) | async-done | bytes 528400 | tf_op jit(solution)/shard_map/psum | solution.py:52
  118.7 1.1 slice.39
  119.7 0.3 copy.31
  120.0 0.1 copy.32
  120.1 1.3 fusion.27
  121.4 15.0 %fusion.31 = f32[64,8192]{1,0:T(8,128)} fusion(bf16[2048,8192]{1,0:T(8,128)(2,1)} %param.10, bf16[8,8,16,128]{3,2,1,0:T(8,128)(2,1)S(1)} %bitcast.16), kind=kOutput, calls=%fused_computation.36 | convolution fusion | flops 2147483648 | bytes 35913728 | tf_op jit(solution)/shard_map/dot_general | solution.py:55
  136.4 0.0 all-reduce.5.cloned.1.call-update
  136.4 86.0 %all-reduce.5.cloned.1.call-done = f32[64,8192]{1,0:T(8,128)} async-done(((f32[64,8192]{1,0:T(8,128)}), f32[64,8192]{1,0:T(8,128)}) %all-reduce.5.cloned.1.call-update) | async-done | bytes 2097168 | tf_op jit(solution)/shard_map/psum | solution.py:56
  222.4 2.7 %fusion.10 = bf16[64,8192]{1,0:T(8,128)(2,1)} fusion(f32[64,8192]{1,0:T(8,128)} %all-reduce.5.cloned.1.call-done, bf16[64,8192]{1,0:T(8,128)(2,1)S(1)} %copy-done.1), kind=kLoop, calls=%fused_computation.16 | loop fusion | flops 1572864 | bytes 4194304 | tf_op jit(solution)/shard_map/convert_element_type | solution.py:57
  (14 shorter events, 0.1 us)
Async XLA Ops:
  7.2 111.5 %all-reduce.3.cloned.1.call-start = ((), (), s32[]{:S(2)}) async-start(), calls=%async_computation | async-start | bytes 2097152 | tf_op jit(solution)/shard_map/psum | solution.py:52
  11.1 17.5 %copy-start.2 = (s32[64]{0:T(128)S(1)}, s32[64]{0:T(128)}, u32[]{:S(2)}) copy-start(s32[64]{0:T(128)} %param.13) | copy-start | bytes 772
  55.4 3.4 %copy-start = (bf16[64,256,2,128]{3,2,1,0:T(2,128)(2,1)}, bf16[64,256,2,128]{3,2,1,0:T(2,128)(2,1)S(1)}, u32[]{:S(2)}) copy-start(bf16[64,256,2,128]{3,2,1,0:T(2,128)(2,1)S(1)} %get-tuple-element.8) | copy-start | bytes 25165828
  81.8 140.6 %all-reduce.5.cloned.1.call-start = ((), (), s32[]{:S(2)}) async-start(), calls=%async_computation.1 | async-start | bytes 4194304 | tf_op jit(solution)/shard_map/psum | solution.py:56
  121.4 101.1 %copy-start.1 = (bf16[64,8192]{1,0:T(8,128)(2,1)S(1)}, bf16[64,8192]{1,0:T(8,128)(2,1)}, u32[]{:S(2)}) copy-start(bf16[64,8192]{1,0:T(8,128)(2,1)} %param.7) | copy-start | bytes 3145732
Sparse Core Ops, SparseCore 0:
  82.0 36.6 all-reduce.2
  136.5 85.8 all-reduce.4
where the time goes:
time: 232 us
  waiting for transfers between devices  123 us (53%)
  matrix products  39.2 us (17%)
  other arithmetic  36.1 us (16%)
  between operations  14.2 us (6%)
  blocking collectives  13.5 us (6%)
  local copies, waits for them, and re-layouts  6.03 us (3%)
    psum x1, waiting for transfers between devices, local_step(): proj_sum = lax.psum(head_part, 'tp')  86 us
    psum x1, waiting for transfers between devices, local_step(): merged = lax.psum(packed, 'sp')  36.6 us
    select_n x1, other arithmetic, local_step(): v_upd = jnp.where(new_row, grouped[:, :, q_per_kv + 1][:, None], v_cache)  25.6 us
    dot_general x1, matrix products, local_step(): jnp.dot(normed, w_qkv, preferred_element_type=jnp.float32)  17.1 us
    dot_general x1, matrix products, local_step(): head_part = jnp.dot(attn_flat, w_out, preferred_element_type=jnp.float32)  15 us
    pmax x1, blocking collectives, local_step(): global_max = lax.pmax(local_max, 'sp')  13.5 us
    dot_general x1, matrix products, local_step(): jnp.einsum('bgqs,bsgd->bgqd', weights.astype(jnp.bfloat16), v_upd, prefer...  4.69 us
  transfers between devices with their start and end apart: 2, of which 2 were waited for; matrix products, arithmetic and copies ran while one was open for 0% of the time, Pallas kernels for 0%

commit v1 on v0

v1 whole, which is shorter than its diff:
```python
import math
import jax
import jax.numpy as jnp
from jax import lax
from jax.experimental import pallas as pl
from jax.experimental.pallas import tpu as pltpu
from jax.sharding import PartitionSpec as P

F32 = jnp.float32
BF16 = jnp.bfloat16
HD = 128
NEG = -3e38
FLOOR = -1e38
MESH_ID = pl.DeviceIdType.MESH
CHUNK = 128


def rope_tables(positions):
    half_dim = HD // 2
    inv_freq = jnp.exp(jnp.arange(half_dim, dtype=F32) * (-2.0 * math.log(500000.0) / HD))
    angles = positions.astype(F32)[:, None] * inv_freq[None, :]
    cos_part, sin_part = jnp.cos(angles), jnp.sin(angles)
    return jnp.concatenate([cos_part, cos_part], axis=-1), jnp.concatenate([-sin_part, sin_part], axis=-1)


def remote(src, dst, send_sem, recv_sem, device_id):
    return pltpu.make_async_remote_copy(
        src_ref=src, dst_ref=dst, send_sem=send_sem, recv_sem=recv_sem, device_id=device_id, device_id_type=MESH_ID
    )


def sp_peers():
    sp = lax.axis_index('sp')
    return sp, sp + 1 - 2 * lax.rem(sp, 2), lax.rem(sp + 2, 4)


def enter(peers):
    barrier = pltpu.get_barrier_semaphore()
    for peer in peers:
        pl.semaphore_signal(barrier, inc=1, device_id=peer, device_id_type=MESH_ID)
    pl.semaphore_wait(barrier, len(peers))


def qkv_kernel(h_ref, scale_ref, cos_ref, sin_ref, w_hbm, kc_hbm, vc_hbm, qkv_ref, k_ref, v_ref,
               w_buf, u_ref, w_sem, c_sem, send_sem, recv_sem):
    sp, partner, cross = sp_peers()
    width = w_buf.shape[1]
    heads = width // HD
    pieces = w_sem.shape[0]
    depth = w_buf.shape[0] // pieces
    col = pl.multiple_of(sp * width, HD)
    w_copies = [
        pltpu.make_async_copy(w_hbm.at[pl.ds(i * depth, depth), pl.ds(col, width)], w_buf.at[pl.ds(i * depth, depth)], w_sem.at[i])
        for i in range(pieces)
    ]
    for copy in w_copies:
        copy.start()
    enter([{'sp': partner}, {'sp': cross}])

    d = h_ref.shape[1]
    x = h_ref[...].astype(F32)
    mean = jnp.sum(x, axis=-1, keepdims=True) * (1.0 / d)
    centered = x - mean
    var = jnp.sum(centered * centered, axis=-1, keepdims=True) * (1.0 / d)
    inv = lax.rsqrt(var + 1e-5)
    u_ref[...] = ((h_ref[...].astype(F32) - mean) * inv * scale_ref[...].astype(F32)).astype(BF16)

    cache_copies = [pltpu.make_async_copy(kc_hbm, k_ref, c_sem.at[0]), pltpu.make_async_copy(vc_hbm, v_ref, c_sem.at[1])]
    acc = None
    for i in range(pieces):
        w_copies[i].wait()
        if i == pieces // 2:
            cache_copies[0].start()
        part = jnp.dot(u_ref[:, i * depth:(i + 1) * depth], w_buf[i * depth:(i + 1) * depth, :], preferred_element_type=F32)
        acc = part if acc is None else acc + part
    cache_copies[1].start()
    proj = jnp.clip(acc.astype(BF16).astype(F32), -8.0, 8.0)
    odd = lax.rem(sp, 2)
    for j in range(heads):
        val = proj[:, j * HD:(j + 1) * HD]
        rot = (val * cos_ref[...] + pltpu.roll(val, HD // 2, 1) * sin_ref[...]).astype(BF16).astype(F32)
        if j == heads - 1:
            rot = jnp.where(odd == 1, val, rot)
        qkv_ref[sp, j] = rot
    to_partner = remote(qkv_ref.at[sp], qkv_ref.at[sp], send_sem.at[0], recv_sem.at[0], {'sp': partner})
    to_cross = remote(qkv_ref.at[sp], qkv_ref.at[sp], send_sem.at[1], recv_sem.at[1], {'sp': cross})
    to_cross.start()
    to_partner.start()
    to_cross.wait_recv()
    forward = remote(qkv_ref.at[cross], qkv_ref.at[cross], send_sem.at[2], recv_sem.at[2], {'sp': partner})
    forward.start()
    to_partner.wait()
    to_cross.wait_send()
    forward.wait()
    for copy in cache_copies:
        copy.wait()


def attention_kernel(pos_ref, qkv_ref, k_ref, v_ref, k_out, v_out, acc_ref, stat_ref, q_ref, out_sem):
    n_seq, rows, _ = k_ref.shape
    seq_local = rows // 2
    group = acc_ref.shape[2]
    base = lax.axis_index('sp') * seq_local
    per_kv = group + 2
    for g in range(2):
        for j in range(group):
            n = g * per_kv + j
            q_ref[pl.ds(g * group + j, n_seq, stride=2 * group), :] = qkv_ref[n]

    tile = 16
    row_id = lax.broadcasted_iota(jnp.int32, (tile, HD), 0)

    def patch(b, carry):
        row = 2 * (pos_ref[b] - base)

        @pl.when((row >= 0) & (row < rows))
        def _():
            start = pl.multiple_of((row // tile) * tile, tile)
            off = row - start
            for ref, slot in ((k_ref, group), (v_ref, group + 1)):
                block = ref[b, pl.ds(start, tile), :].astype(F32)
                first = qkv_ref[slot, pl.ds(b, 1), :]
                second = qkv_ref[per_kv + slot, pl.ds(b, 1), :]
                block = jnp.where(row_id == off, first, jnp.where(row_id == off + 1, second, block))
                ref[b, pl.ds(start, tile), :] = block.astype(BF16)

        return carry

    lax.fori_loop(0, n_seq, patch, 0)
    pieces = out_sem.shape[1]
    span = n_seq // pieces
    copies = []
    for i in range(pieces):
        for s, (src, dst) in enumerate(((k_ref, k_out), (v_ref, v_out))):
            copy = pltpu.make_async_copy(src.at[pl.ds(i * span, span)], dst.at[pl.ds(i * span, span)], out_sem.at[s, i])
            copy.start()
            copies.append(copy)

    n_q = 2 * group
    col_id = lax.broadcasted_iota(jnp.int32, (n_q, rows), 1)
    head_id = lax.broadcasted_iota(jnp.int32, (n_q, rows), 0) // group
    col_key = jnp.where(lax.rem(col_id, 2) == head_id, col_id, 1 << 30)
    lane = lax.broadcasted_iota(jnp.int32, (n_q, HD), 1)
    factor = HD ** -0.5 * math.log2(math.e)
    unroll = 4

    def step(i, stats):
        results = []
        for r in range(unroll):
            b = i * unroll + r
            limit = 2 * (pos_ref[b] - base + 1)
            q = q_ref[pl.ds(pl.multiple_of(b * n_q, n_q), n_q), :].astype(BF16)
            scores = lax.dot_general(q, k_ref[b], (((1,), (1,)), ((), ())), preferred_element_type=F32) * factor
            scores = jnp.where(col_key < limit, scores, NEG)
            top = jnp.maximum(jnp.max(scores, axis=-1, keepdims=True), FLOOR)
            probs = jnp.exp2(scores - top)
            total = jnp.sum(probs, axis=-1, keepdims=True)
            out = jnp.dot(probs.astype(BF16), v_ref[b], preferred_element_type=F32)
            results.append((b, top, total, out))
        for b, top, total, out in results:
            acc_ref[0, b] = out[:group]
            acc_ref[1, b] = out[group:]
            stats = jnp.where(lane == b, top, jnp.where(lane == b + n_seq, total, stats))
        return stats

    stats = lax.fori_loop(0, n_seq // unroll, step, jnp.zeros((n_q, HD), F32))
    stat_ref[0] = stats[:group]
    stat_ref[1] = stats[group:]
    for copy in copies:
        copy.wait()


def project_kernel(h_ref, acc_ref, stat_ref, w_hbm, out_ref, w_buf, d_acc, d_stat, m_acc, m_stat, y_acc, y_stat, att, a_ref,
                   part, e_buf, a_buf, b_buf, tot, y_buf, p1_buf, p2_buf,
                   w_sem, st_send, st_recv, d_send, d_recv, y_send, y_recv, g_send, g_recv,
                   e_send, e_recv, b_send, b_recv, t_send, t_recv, ys, yr, p1s, p1r, p2s, p2r):
    sp, partner, cross = sp_peers()
    core = lax.rem(sp, 2)
    z = lax.axis_index('tp')
    is_hub = (z == 1) | (z == 2)
    end_of_hub = 3 * (z - 1)
    hub_of_end = 1 + z // 2
    other_hub = 3 - z
    n_seq = h_ref.shape[0]
    width = w_buf.shape[1]
    col = pl.multiple_of(sp * width, HD)
    w_copy = pltpu.make_async_copy(w_hbm.at[:, pl.ds(col, width)], w_buf, w_sem)
    w_copy.start()

    barrier = pltpu.get_barrier_semaphore()
    for peer in ({'sp': partner}, {'sp': cross}):
        pl.semaphore_signal(barrier, inc=1, device_id=peer, device_id_type=MESH_ID)

    @pl.when(is_hub)
    def _():
        for peer in ({'tp': end_of_hub}, {'tp': other_hub}):
            pl.semaphore_signal(barrier, inc=1, device_id=peer, device_id_type=MESH_ID)
        pl.semaphore_wait(barrier, 4)

    @pl.when(jnp.logical_not(is_hub))
    def _():
        pl.semaphore_signal(barrier, inc=1, device_id={'tp': hub_of_end}, device_id_type=MESH_ID)
        pl.semaphore_wait(barrier, 3)

    group = stat_ref.shape[1]
    blocks = d_send.shape[0]
    span = n_seq // blocks
    height = span * group
    other = 1 - core
    st_copy = remote(stat_ref.at[other], d_stat, st_send.at[0], st_recv.at[0], {'sp': partner})
    st_copy.start()
    d_copies = []
    for i in range(blocks):
        copy = remote(acc_ref.at[other, pl.ds(i * height, height)], d_acc.at[pl.ds(i * height, height)],
                      d_send.at[i], d_recv.at[i], {'sp': partner})
        copy.start()
        d_copies.append(copy)
    st_copy.wait_recv()
    lane = lax.broadcasted_iota(jnp.int32, (group, HD), 1)

    def weights(s0, s1):
        l0, l1 = pltpu.roll(s0, HD // 2, 1), pltpu.roll(s1, HD // 2, 1)
        top = jnp.maximum(s0, s1)
        e0, e1 = jnp.exp2(s0 - top), jnp.exp2(s1 - top)
        return top, e0, e1, l0 * e0 + l1 * e1

    top, e0, e1, total = weights(stat_ref[core], d_stat[...])
    m_stat[...] = jnp.where(lane < HD // 2, top, pltpu.roll(total, HD // 2, 1))
    sy_copy = remote(m_stat, y_stat, st_send.at[1], st_recv.at[1], {'sp': cross})
    y_copies = []
    for i in range(blocks):
        d_copies[i].wait_recv()
        for r in range(span):
            b = i * span + r
            rows = pl.ds(b * group, group)
            m_acc[rows, :] = acc_ref[core, rows, :] * e0[:, b:b + 1] + d_acc[rows, :] * e1[:, b:b + 1]
        if i == 0:
            sy_copy.start()
        copy = remote(m_acc.at[pl.ds(i * height, height)], y_acc.at[pl.ds(i * height, height)],
                      y_send.at[i], y_recv.at[i], {'sp': cross})
        copy.start()
        y_copies.append(copy)
    sy_copy.wait_recv()
    top, e0, e1, total = weights(m_stat[...], y_stat[...])
    share = 1.0 / jnp.where(lane < HD // 2, total, 1.0)
    e0, e1 = e0 * share, e1 * share
    g_copies = []
    for i in range(blocks):
        y_copies[i].wait_recv()
        for r in range(span):
            b = i * span + r
            rows = pl.ds(b * group, group)
            val = m_acc[rows, :] * e0[:, b:b + 1] + y_acc[rows, :] * e1[:, b:b + 1]
            att[core, rows, :] = val.astype(BF16).astype(F32)
        copy = remote(att.at[core, pl.ds(i * height, height)], att.at[core, pl.ds(i * height, height)],
                      g_send.at[i], g_recv.at[i], {'sp': partner})
        copy.start()
        g_copies.append(copy)
    for i in range(blocks):
        g_copies[i].wait_recv()
    for g in range(2):
        for j in range(group):
            n = g * group + j
            a_ref[:, n * HD:(n + 1) * HD] = att[g, pl.ds(j, n_seq, stride=group), :].astype(BF16)
    w_copy.wait()

    chunks = part.shape[0]
    wide = 2 * CHUNK

    def compute(j):
        val = jnp.dot(a_ref[...], w_buf[:, j * wide:(j + 1) * wide], preferred_element_type=F32)
        part[2 * j] = val[:, :CHUNK]
        part[2 * j + 1] = val[:, CHUNK:]

    def emit(block, i, ref):
        at = pl.ds(pl.multiple_of(block * width + i * CHUNK, CHUNK), CHUNK)
        out_ref[:, at] = (h_ref[:, at].astype(F32) + ref[i]).astype(BF16)

    def e_copy(i):
        return remote(part.at[i], e_buf.at[i], e_send.at[i], e_recv.at[i], {'tp': hub_of_end})

    def b_copy(i):
        return remote(a_buf.at[i], b_buf.at[i], b_send.at[i], b_recv.at[i], {'tp': other_hub})

    def t_copy(i):
        return remote(tot.at[i], tot.at[i], t_send.at[i], t_recv.at[i], {'tp': end_of_hub})

    def y_copy(i):
        return remote(tot.at[i], y_buf.at[i], ys.at[i], yr.at[i], {'sp': cross})

    def p1_copy(i):
        return remote(tot.at[i], p1_buf.at[i], p1s.at[i], p1r.at[i], {'sp': partner})

    def p2_copy(i):
        return remote(y_buf.at[i], p2_buf.at[i], p2s.at[i], p2r.at[i], {'sp': partner})

    far = lax.rem(partner + 2, 4)

    def spread(i):
        y_copy(i).start()
        p1_copy(i).start()
        emit(sp, i, tot)

    def pass_on(i):
        y_copy(i).wait_recv()
        p2_copy(i).start()
        emit(cross, i, y_buf)

    @pl.when(is_hub)
    def _():
        lag, lag2 = 3, 6
        for j in range(chunks // 2):
            compute(j)
        for t in range(chunks + lag2):
            if t < chunks:
                e_copy(t).wait_recv()
                a_buf[t] = part[t] + e_buf[t]
                b_copy(t).start()
            i = t - lag
            if 0 <= i < chunks:
                b_copy(i).wait_recv()
                tot[i] = a_buf[i] + b_buf[i]
                t_copy(i).start()
                spread(i)
            i = t - lag2
            if 0 <= i < chunks:
                pass_on(i)
        for i in range(chunks):
            b_copy(i).wait_send()
            t_copy(i).wait_send()

    @pl.when(jnp.logical_not(is_hub))
    def _():
        lag = 3
        for j in range(chunks // 2):
            compute(j)
            e_copy(2 * j).start()
            e_copy(2 * j + 1).start()
        for t in range(chunks + lag):
            if t < chunks:
                t_copy(t).wait_recv()
                spread(t)
            i = t - lag
            if 0 <= i < chunks:
                pass_on(i)
        for i in range(chunks):
            e_copy(i).wait_send()

    for i in range(chunks):
        p1_copy(i).wait_recv()
        emit(partner, i, p1_buf)
        p2_copy(i).wait_recv()
        emit(far, i, p2_buf)
    for i in range(chunks):
        y_copy(i).wait_send()
        p1_copy(i).wait_send()
        p2_copy(i).wait_send()
    st_copy.wait_send()
    sy_copy.wait_send()
    for i in range(blocks):
        d_copies[i].wait_send()
        y_copies[i].wait_send()
        g_copies[i].wait_send()


def solution(mesh):
    cache_spec = P('dp', 'sp', 'tp', None)
    hbm = pl.BlockSpec(memory_space=pltpu.HBM)
    vmem = pl.BlockSpec(memory_space=pltpu.VMEM)
    smem = pl.BlockSpec(memory_space=pltpu.SMEM)
    dma = pltpu.SemaphoreType.DMA

    def local_step(hidden, norm_scale, w_qkv, w_out, k_cache, v_cache, positions):
        n_seq, seq_local, kv_local, head_dim = k_cache.shape
        d = hidden.shape[1]
        rows = seq_local * kv_local
        heads = w_qkv.shape[1] // head_dim
        group = heads // kv_local - 2
        k_flat = k_cache.reshape(n_seq, rows, head_dim)
        v_flat = v_cache.reshape(n_seq, rows, head_dim)
        cos_tab, sin_tab = rope_tables(positions)
        share = heads // 4
        cache_type = pltpu.VMEM((n_seq, rows, head_dim), BF16)
        qkv, k_vmem, v_vmem = pl.pallas_call(
            qkv_kernel,
            out_shape=[pltpu.VMEM((4, share, n_seq, head_dim), F32), cache_type, cache_type],
            in_specs=[vmem, vmem, vmem, vmem, hbm, hbm, hbm],
            out_specs=[vmem, vmem, vmem],
            scratch_shapes=[
                pltpu.VMEM((d, share * head_dim), BF16), pltpu.VMEM((n_seq, d), BF16),
                dma((8,)), dma((2,)), dma((3,)), dma((3,)),
            ],
            compiler_params=pltpu.CompilerParams(collective_id=0, has_side_effects=True, vmem_limit_bytes=24 << 20),
            name='qkv',
        )(hidden, norm_scale.reshape(1, d), cos_tab, sin_tab, *[pltpu.with_memory_space_constraint(a, pltpu.HBM) for a in (w_qkv, k_flat, v_flat)])
        qkv = qkv.reshape(heads, n_seq, head_dim)

        k_out, v_out, acc, stat = pl.pallas_call(
            attention_kernel,
            out_shape=[
                jax.ShapeDtypeStruct(k_flat.shape, BF16), jax.ShapeDtypeStruct(v_flat.shape, BF16),
                pltpu.VMEM((2, n_seq, group, head_dim), F32), pltpu.VMEM((2, group, head_dim), F32),
            ],
            in_specs=[smem, vmem, vmem, vmem],
            out_specs=[hbm, hbm, vmem, vmem],
            scratch_shapes=[pltpu.VMEM((n_seq * 2 * group, head_dim), F32), dma((2, 8))],
            compiler_params=pltpu.CompilerParams(vmem_limit_bytes=16 << 20),
            name='attention',
        )(positions, qkv, k_vmem, v_vmem)
        acc = acc.reshape(2, n_seq * group, head_dim)

        width = d // 4
        depth = w_out.shape[0]
        chunks = width // CHUNK
        blocks = 4
        slot = pltpu.VMEM((chunks, n_seq, CHUNK), F32)
        half = pltpu.VMEM((n_seq * group, head_dim), F32)
        tile = pltpu.VMEM((group, head_dim), F32)
        h_out = pl.pallas_call(
            project_kernel,
            out_shape=jax.ShapeDtypeStruct((n_seq, d), BF16),
            in_specs=[vmem, vmem, vmem, hbm],
            out_specs=vmem,
            scratch_shapes=[
                pltpu.VMEM((depth, width), BF16), half, tile, half, tile, half, tile,
                pltpu.VMEM((2, n_seq * group, head_dim), F32), pltpu.VMEM((n_seq, depth), BF16),
                slot, slot, slot, slot, slot, slot, slot, slot,
                dma(()), dma((2,)), dma((2,)), dma((blocks,)), dma((blocks,)), dma((blocks,)), dma((blocks,)),
                dma((blocks,)), dma((blocks,)),
                *[dma((chunks,)) for _ in range(12)],
            ],
            compiler_params=pltpu.CompilerParams(collective_id=1, has_side_effects=True, vmem_limit_bytes=40 << 20),
            name='project',
        )(hidden, acc, stat, pltpu.with_memory_space_constraint(w_out, pltpu.HBM))
        return h_out, k_out.reshape(k_cache.shape), v_out.reshape(v_cache.shape)

    return jax.shard_map(
        local_step,
        mesh=mesh,
        in_specs=(P('dp', None), P(None), P(None, 'tp'), P('tp', None), cache_spec, cache_spec, P('dp')),
        out_specs=(P('dp', None), cache_spec, cache_spec),
        check_vma=False,
    )
```

time: 232 us -> 77.7 us (0.33)
  waiting for transfers between devices: 123 us -> 0 us
  Pallas kernels: 0 us -> 72.8 us
  matrix products: 39.2 us -> 0 us
  other arithmetic: 36.1 us -> 0.95 us
  blocking collectives: 13.5 us -> 0 us
  between operations: 14.2 us -> 0.7 us
  local copies, waits for them, and re-layouts: 6.03 us -> 2.94 us
    psum x2 -> x0, waiting for transfers between devices: 123 us -> none  [the longest x1 86 us: local_step(): proj_sum = lax.psum(head_part, 'tp')]
    pallas_call x0 -> x3, Pallas kernels: none -> 72.8 us  [the longest x1 40.6 us: local_step(): pl.pallas_call(project_kernel, out_shape=jax.ShapeDtypeStruct((n_seq, d),...]
    dot_general x4 -> x0, matrix products: 39.2 us -> none  [the longest x1 17.1 us: local_step(): jnp.dot(normed, w_qkv, preferred_element_type=jnp.float32)]
    select_n x1 -> x0, other arithmetic: 25.6 us -> none  [local_step(): v_upd = jnp.where(new_row, grouped[:, :, q_per_kv + 1][:, None], v_cache)]
    pmax x1 -> x0, blocking collectives: 13.5 us -> none  [local_step(): global_max = lax.pmax(local_max, 'sp')]
    convert_element_type x5 -> x1, other arithmetic: 4.86 us -> 0.66 us  [rope_tables(): angles = positions.astype(F32)[:, None] * inv_freq[None, :]]
    reduce_sum x3 -> x0, other arithmetic: 3.54 us -> none  [the longest x1 1.67 us: layer_norm_bf16(): row_var = jnp.mean(centered * centered, axis=-1, keepdims=True)]
  transfers between devices with their start and end apart: 2 -> 0, of which waited for: 2 -> 0; matrix products, arithmetic and copies ran while one was open for 0% -> 0% of each run, Pallas kernels for 0% -> 0%
where the time goes in v1:
time: 77.7 us; the launch traced here: 77.4 us
  Pallas kernels  72.8 us (94%)
  local copies, waits for them, and re-layouts  2.94 us (4%)
  other arithmetic  0.95 us (1%)
    pallas_call x1, Pallas kernels, local_step(): pl.pallas_call(project_kernel, out_shape=jax.ShapeDtypeStruct((n_seq, d),...  40.6 us
    pallas_call x1, Pallas kernels, local_step(): pl.pallas_call(attention_kernel, out_shape=[jax.ShapeDtypeStruct(k_flat.s...  19.3 us
    pallas_call x1, Pallas kernels, local_step(): pl.pallas_call(qkv_kernel, out_shape=[pltpu.VMEM((4, share, n_seq, head_d...  12.9 us
    unnamed x7, local copies, waits for them, and re-layouts  2.2 us

profile of v1, /device:TPU:0, one launch (start us, length us, event | category | flops | bytes accessed | tf_op | source)
XLA Modules:
  0.0 77.4 jit_solution(15414158469323996344)
XLA Ops:
  0.6 0.7 convert_element_type.3
  1.3 0.7 reshape.33.scale_ref
  2.0 0.2 fusion
  2.2 0.1 pad_maximum_fusion
  2.3 0.0 copy-start
  2.3 1.2 %copy-done = bf16[64,8192]{1,0:T(8,128)(2,1)S(1)} copy-done((bf16[64,8192]{1,0:T(8,128)(2,1)S(1)}, bf16[64,8192]{1,0:T(8,128)(2,1)}, u32[]{:S(2)}) %copy-start) | copy-done | bytes 1048600
  3.6 0.0 copy-start.2
  3.6 12.9 %qkv.1 = (f32[4,5,64,128]{3,2,1,0:T(8,128)S(1)}, bf16[64,512,128]{2,1,0:T(8,128)(2,1)S(1)}, bf16[64,512,128]{2,1,0:T(8,128)(2,1)S(1)}) custom-call(bf16[64,8192]{1,0:T(8,128)(2,1)S(1)} %copy-done, bf16[1,8192]{1,0:T(2,128)(2,1)S(1)} %reshape.33.scale_ref, f32[64,128]{1,0:T(8,128)S(1)} %get-tuple-element.20.cos_ref, f32[64,128]{1,0:T(8,128)S(1)} %get-tuple-element.21.sin_ref, ...), custom_call_target="tpu_custom_call" | custom-call | tf_op jit(solution)/shard_map/qkv/pallas_call | solution.py:384
  16.5 0.0 copy-done.2
  16.5 0.0 copy-start.1
  16.5 19.3 %attention.1 = (bf16[64,512,128]{2,1,0:T(8,128)(2,1)}, bf16[64,512,128]{2,1,0:T(8,128)(2,1)}, f32[2,64,8,128]{3,2,1,0:T(8,128)S(1)}, f32[2,8,128]{2,1,0:T(8,128)S(1)}) custom-call(s32[64]{0:T(128)S(1)} %copy-done.2, f32[20,64,128]{2,1,0:T(8,128)S(1)} %bitcast.6, bf16[64,512,128]{2,1,0:T(8,128)(2,1)S(1)} %get-tuple-element.11.k_ref, ...), custom_call_target="tpu_custom_call" | custom-call | tf_op jit(solution)/shard_map/attention/pallas_call | solution.py:398
  35.8 0.0 copy-done.1
  35.8 40.6 %project.1 = bf16[64,8192]{1,0:T(8,128)(2,1)S(1)} custom-call(bf16[64,8192]{1,0:T(8,128)(2,1)S(1)} %copy-done.1, f32[2,512,128]{2,1,0:T(8,128)S(1)} %bitcast.7, f32[2,8,128]{2,1,0:T(8,128)S(1)} %get-tuple-element.14.stat_ref, bf16[2048,8192]{1,0:T(8,128)(2,1)} %w_hbm.3), custom_call_target="tpu_custom_call" | custom-call | tf_op jit(solution)/shard_map/project/pallas_call | solution.py:419
  76.4 1.0 %copy.11 = bf16[64,8192]{1,0:T(8,128)(2,1)} copy(bf16[64,8192]{1,0:T(8,128)(2,1)S(1)} %project.1) | data formatting | bytes 2097152
  (1 shorter events, 0.0 us)
Async XLA Ops:
  2.3 1.2 %copy-start = (bf16[64,8192]{1,0:T(8,128)(2,1)S(1)}, bf16[64,8192]{1,0:T(8,128)(2,1)}, u32[]{:S(2)}) copy-start(bf16[64,8192]{1,0:T(8,128)(2,1)} %h_ref.3) | copy-start | bytes 3145732
  3.6 13.0 %copy-start.2 = (s32[64]{0:T(128)S(1)}, s32[64]{0:T(128)}, u32[]{:S(2)}) copy-start(s32[64]{0:T(128)} %pos_ref.1) | copy-start | bytes 772
  16.5 19.3 %copy-start.1 = (bf16[64,8192]{1,0:T(8,128)(2,1)S(1)}, bf16[64,8192]{1,0:T(8,128)(2,1)}, u32[]{:S(2)}) copy-start(bf16[64,8192]{1,0:T(8,128)(2,1)} %h_ref.3) | copy-start | bytes 3145732

commit v2 on v1

v2 whole, which is shorter than its diff:
```python
import math
import jax
import jax.numpy as jnp
from jax import lax
from jax.experimental import pallas as pl
from jax.experimental.pallas import tpu as pltpu
from jax.sharding import PartitionSpec as P

F32 = jnp.float32
BF16 = jnp.bfloat16
HD = 128
NEG = -3e38
FLOOR = -1e38
MESH_ID = pl.DeviceIdType.MESH
CHUNK = 128


def remote(src, dst, send_sem, recv_sem, device_id):
    return pltpu.make_async_remote_copy(
        src_ref=src, dst_ref=dst, send_sem=send_sem, recv_sem=recv_sem, device_id=device_id, device_id_type=MESH_ID
    )


def sp_peers():
    sp = lax.axis_index('sp')
    return sp, sp + 1 - 2 * lax.rem(sp, 2), lax.rem(sp + 2, 4)


def enter(peers):
    barrier = pltpu.get_barrier_semaphore()
    for peer in peers:
        pl.semaphore_signal(barrier, inc=1, device_id=peer, device_id_type=MESH_ID)
    pl.semaphore_wait(barrier, len(peers))


def qkv_kernel(h_hbm, scale_hbm, pos_hbm, w_hbm, kc_hbm, vc_hbm, qkv_ref, k_ref, v_ref,
               h_ref, scale_ref, pos_ref, w0_buf, w1_buf, w2_buf, u_ref, cos_ref, sin_ref,
               i_sem, w_sem, c_sem, a_send, a_recv, b_send, b_recv, f_send, f_recv):
    sp, partner, cross = sp_peers()
    n_seq, d = h_ref.shape
    ins = [pltpu.make_async_copy(src, dst, i_sem.at[i])
           for i, (src, dst) in enumerate(((pos_hbm, pos_ref), (h_hbm, h_ref), (scale_hbm, scale_ref)))]
    for copy in ins:
        copy.start()
    bufs = (w0_buf, w1_buf, w2_buf)
    width = sum(buf.shape[1] for buf in bufs)
    pieces = w_sem.shape[1]
    depth = d // pieces
    w_copies, first = [], 0
    for g, buf in enumerate(bufs):
        col = pl.multiple_of(sp * width + first, HD)
        first += buf.shape[1]
        group = []
        for i in range(pieces):
            rows = pl.ds(i * depth, depth)
            copy = pltpu.make_async_copy(w_hbm.at[rows, pl.ds(col, buf.shape[1])], buf.at[rows], w_sem.at[g, i])
            copy.start()
            group.append(copy)
        w_copies.append(group)
    enter([{'sp': partner}, {'sp': cross}])

    ins[0].wait()
    row_id = lax.broadcasted_iota(jnp.int32, (n_seq, n_seq), 0)
    col_id = lax.broadcasted_iota(jnp.int32, (n_seq, n_seq), 1)
    pos = jnp.sum(jnp.where(row_id == col_id, pos_ref[...].astype(F32), 0.0), axis=-1, keepdims=True)
    lane = lax.broadcasted_iota(jnp.int32, (n_seq, HD), 1)
    freq = lax.rem(lane, HD // 2).astype(F32)
    angles = pos * jnp.exp(freq * (-2.0 * math.log(500000.0) / HD))
    cos_ref[...] = jnp.cos(angles)
    sin_part = jnp.sin(angles)
    sin_ref[...] = jnp.where(lane < HD // 2, -sin_part, sin_part)

    ins[1].wait()
    tiles = d // HD

    def tile(k):
        return h_ref[:, k * HD:(k + 1) * HD].astype(F32)

    total = tile(0)
    for k in range(1, tiles):
        total += tile(k)
    mean = jnp.sum(total, axis=-1, keepdims=True) * (1.0 / d)
    total = jnp.zeros((n_seq, HD), F32)
    for k in range(tiles):
        centered = tile(k) - mean
        total += centered * centered
    inv = lax.rsqrt(jnp.sum(total, axis=-1, keepdims=True) * (1.0 / d) + 1e-5)
    ins[2].wait()
    scale_rows = scale_ref[...].astype(F32)
    for k in range(tiles):
        u_ref[:, k * HD:(k + 1) * HD] = ((tile(k) - mean) * inv * scale_rows[k:k + 1, :]).astype(BF16)

    cache_copies = [pltpu.make_async_copy(kc_hbm, k_ref, c_sem.at[0]), pltpu.make_async_copy(vc_hbm, v_ref, c_sem.at[1])]
    odd = lax.rem(sp, 2)
    heads = width // HD
    to_cross, to_partner, forward = [], [], []
    j = 0
    for g, buf in enumerate(bufs):
        acc = None
        for i in range(pieces):
            w_copies[g][i].wait()
            rows = slice(i * depth, (i + 1) * depth)
            part = jnp.dot(u_ref[:, rows], buf[rows, :], preferred_element_type=F32)
            acc = part if acc is None else acc + part
        if g >= 1:
            cache_copies[g - 1].start()
        proj = jnp.clip(acc.astype(BF16).astype(F32), -8.0, 8.0)
        n = buf.shape[1] // HD
        for r in range(n):
            val = proj[:, r * HD:(r + 1) * HD]
            rot = (val * cos_ref[...] + pltpu.roll(val, HD // 2, 1) * sin_ref[...]).astype(BF16).astype(F32)
            if j + r == heads - 1:
                rot = jnp.where(odd == 1, val, rot)
            qkv_ref[sp, j + r] = rot
        mine = qkv_ref.at[sp, pl.ds(j, n)]
        theirs = qkv_ref.at[cross, pl.ds(j, n)]
        to_cross.append(remote(mine, mine, a_send.at[g], a_recv.at[g], {'sp': cross}))
        to_partner.append(remote(mine, mine, b_send.at[g], b_recv.at[g], {'sp': partner}))
        forward.append(remote(theirs, theirs, f_send.at[g], f_recv.at[g], {'sp': partner}))
        to_cross[g].start()
        to_partner[g].start()
        j += n
    for g in range(len(bufs)):
        to_cross[g].wait_recv()
        forward[g].start()
    for copy in cache_copies:
        copy.wait()
    for g in range(len(bufs)):
        to_partner[g].wait()
        to_cross[g].wait_send()
        forward[g].wait()


def attention_kernel(pos_ref, qkv_ref, k_ref, v_ref, k_out, v_out, acc_ref, stat_ref, q_ref, s_ref, p_ref, out_sem):
    n_seq, rows, _ = k_ref.shape
    seq_local = rows // 2
    group = acc_ref.shape[2]
    base = lax.axis_index('sp') * seq_local
    per_kv = group + 2
    n_q = 2 * group

    tile = 16
    row_id = lax.broadcasted_iota(jnp.int32, (tile, HD), 0)
    at_once = 8

    def patch(i, carry):
        for r in range(at_once):
            b = i * at_once + r
            row = 2 * (pos_ref[b] - base)
            start = pl.multiple_of(jnp.clip(row // tile, 0, rows // tile - 1) * tile, tile)
            off = row - start
            for ref, slot in ((k_ref, group), (v_ref, group + 1)):
                block = ref[b, pl.ds(start, tile), :].astype(F32)
                one = qkv_ref[slot, pl.ds(b, 1), :]
                two = qkv_ref[per_kv + slot, pl.ds(b, 1), :]
                block = jnp.where(row_id == off, one, jnp.where(row_id == off + 1, two, block))
                ref[b, pl.ds(start, tile), :] = block.astype(BF16)
        return carry

    lax.fori_loop(0, n_seq // at_once, patch, 0)
    pieces = out_sem.shape[1]
    span = n_seq // pieces
    copies = []
    for i in range(pieces):
        for s, (src, dst) in enumerate(((k_ref, k_out), (v_ref, v_out))):
            copy = pltpu.make_async_copy(src.at[pl.ds(i * span, span)], dst.at[pl.ds(i * span, span)], out_sem.at[s, i])
            copy.start()
            copies.append(copy)
    for g in range(2):
        for j in range(group):
            q_ref[pl.ds(g * group + j, n_seq, stride=n_q), :] = qkv_ref[g * per_kv + j]

    col_id = lax.broadcasted_iota(jnp.int32, (n_q, rows), 1)
    head_id = lax.broadcasted_iota(jnp.int32, (n_q, rows), 0) // group
    col_key = jnp.where(lax.rem(col_id, 2) == head_id, col_id, 1 << 30)
    lane = lax.broadcasted_iota(jnp.int32, (n_q, HD), 1)
    upper = lax.broadcasted_iota(jnp.int32, (2 * n_q, HD), 0) < n_q
    factor = HD ** -0.5 * math.log2(math.e)
    pairs = s_ref.shape[0] // (2 * n_q)
    batch = 2 * pairs

    def score(i):
        for r in range(pairs):
            b = i * batch + 2 * r
            q = q_ref[pl.ds(pl.multiple_of(b * n_q, 2 * n_q), 2 * n_q), :]
            lhs = jnp.concatenate([jnp.where(upper, q, 0.0), jnp.where(upper, 0.0, q)], axis=1).astype(BF16)
            rhs = jnp.concatenate([k_ref[b], k_ref[b + 1]], axis=1)
            out = lax.dot_general(lhs, rhs, (((1,), (1,)), ((), ())), preferred_element_type=F32)
            for e in range(2):
                limit = 2 * (pos_ref[b + e] - base + 1)
                half = out[e * n_q:(e + 1) * n_q] * factor
                s_ref[(2 * r + e) * n_q:(2 * r + e + 1) * n_q, :] = jnp.where(col_key < limit, half, NEG)

    def soften(i, stats):
        for r in range(batch):
            b = i * batch + r
            scores = s_ref[r * n_q:(r + 1) * n_q, :]
            top = jnp.maximum(jnp.max(scores, axis=-1, keepdims=True), FLOOR)
            probs = jnp.exp2(scores - top)
            total = jnp.sum(probs, axis=-1, keepdims=True)
            p_ref[r * n_q:(r + 1) * n_q, :] = probs.astype(BF16)
            stats = jnp.where(lane == b, top, jnp.where(lane == b + n_seq, total, stats))
        return stats

    def weigh(i):
        for r in range(pairs):
            b = i * batch + 2 * r
            rhs = jnp.concatenate([v_ref[b], v_ref[b + 1]], axis=1)
            out = jnp.dot(p_ref[2 * r * n_q:(2 * r + 2) * n_q, :], rhs, preferred_element_type=F32)
            for e in range(2):
                own = out[e * n_q:(e + 1) * n_q, e * HD:(e + 1) * HD]
                acc_ref[0, b + e] = own[:group]
                acc_ref[1, b + e] = own[group:]

    steps = n_seq // batch
    stats = jnp.zeros((n_q, HD), F32)
    score(0)
    stats = soften(0, stats)
    score(1)

    def step(i, stats):
        weigh(i)
        stats = soften(i + 1, stats)
        score(i + 2)
        return stats

    stats = lax.fori_loop(0, steps - 2, step, stats)
    weigh(steps - 2)
    stats = soften(steps - 1, stats)
    weigh(steps - 1)
    stat_ref[0] = stats[:group]
    stat_ref[1] = stats[group:]
    for copy in copies:
        copy.wait()


def project_kernel(h_ref, acc_ref, stat_ref, w_hbm, out_ref, w_buf, d_acc, d_stat, m_acc, m_stat, y_acc, y_stat, att, a_ref,
                   part, e_buf, a_buf, b_buf, tot, y_buf, p1_buf, p2_buf,
                   w_sem, st_send, st_recv, d_send, d_recv, y_send, y_recv, g_send, g_recv,
                   e_send, e_recv, b_send, b_recv, t_send, t_recv, ys, yr, p1s, p1r, p2s, p2r):
    sp, partner, cross = sp_peers()
    core = lax.rem(sp, 2)
    y = sp // 2
    z = lax.axis_index('tp')
    is_hub = (z == 1) | (z == 2)
    end_of_hub = 3 * (z - 1)
    hub_of_end = 1 + z // 2
    other_hub = 3 - z
    width = w_buf.shape[1]
    col = pl.multiple_of(core * width, HD)
    w_copy = pltpu.make_async_copy(w_hbm.at[:, pl.ds(col, width)], w_buf, w_sem)
    w_copy.start()

    barrier = pltpu.get_barrier_semaphore()
    for peer in ({'sp': partner}, {'sp': cross}):
        pl.semaphore_signal(barrier, inc=1, device_id=peer, device_id_type=MESH_ID)

    @pl.when(is_hub)
    def _():
        for peer in ({'tp': end_of_hub}, {'tp': other_hub}):
            pl.semaphore_signal(barrier, inc=1, device_id=peer, device_id_type=MESH_ID)
        pl.semaphore_wait(barrier, 4)

    @pl.when(jnp.logical_not(is_hub))
    def _():
        pl.semaphore_signal(barrier, inc=1, device_id={'tp': hub_of_end}, device_id_type=MESH_ID)
        pl.semaphore_wait(barrier, 3)

    group = stat_ref.shape[1]
    seqs = out_ref.shape[0] // 2
    blocks = y_send.shape[0]
    span = seqs // blocks
    height = span * group
    other = 1 - core
    st_copy = remote(stat_ref.at[other], d_stat, st_send.at[0], st_recv.at[0], {'sp': partner})
    st_copy.start()

    def rows_of(half, i):
        return pl.ds(pl.multiple_of((half * blocks + i) * height, height), height)

    d_copies = []
    for n in range(2 * blocks):
        rows = rows_of(1 - y if n < blocks else y, n % blocks)
        copy = remote(acc_ref.at[other, rows], d_acc.at[rows], d_send.at[n], d_recv.at[n], {'sp': partner})
        copy.start()
        d_copies.append(copy)
    st_copy.wait_recv()
    lane = lax.broadcasted_iota(jnp.int32, (group, HD), 1)

    def weights(s0, s1):
        l0, l1 = pltpu.roll(s0, HD // 2, 1), pltpu.roll(s1, HD // 2, 1)
        top = jnp.maximum(s0, s1)
        e0, e1 = jnp.exp2(s0 - top), jnp.exp2(s1 - top)
        return top, e0, e1, l0 * e0 + l1 * e1

    def lanes_of(half, val):
        return jnp.where(half == 0, val, pltpu.roll(val, HD - seqs, 1))

    top, e0, e1, total = weights(stat_ref[core], d_stat[...])
    m_stat[...] = jnp.where(lane < HD // 2, top, pltpu.roll(total, HD // 2, 1))
    sy_copy = remote(m_stat, y_stat, st_send.at[1], st_recv.at[1], {'sp': cross})
    y_copies = []
    for n in range(2 * blocks):
        half, i = (1 - y if n < blocks else y), n % blocks
        d_copies[n].wait_recv()
        f0, f1 = lanes_of(half, e0), lanes_of(half, e1)
        first = half * seqs * group
        for r in range(span):
            b = i * span + r
            rows = pl.ds(pl.multiple_of(first + b * group, group), group)
            m_acc[rows, :] = acc_ref[core, rows, :] * f0[:, b:b + 1] + d_acc[rows, :] * f1[:, b:b + 1]
        if n == 0:
            sy_copy.start()
        if n < blocks:
            copy = remote(m_acc.at[rows_of(half, i)], y_acc.at[pl.ds(i * height, height)], y_send.at[i], y_recv.at[i], {'sp': cross})
            copy.start()
            y_copies.append(copy)
    sy_copy.wait_recv()
    top, e0, e1, total = weights(m_stat[...], y_stat[...])
    share = 1.0 / jnp.where(lane < HD // 2, total, 1.0)
    e0, e1 = lanes_of(y, e0 * share), lanes_of(y, e1 * share)
    first = y * seqs * group
    g_copies = []
    for i in range(blocks):
        y_copies[i].wait_recv()
        for r in range(span):
            b = i * span + r
            rows = pl.ds(b * group, group)
            mine = m_acc[pl.ds(pl.multiple_of(first + b * group, group), group), :]
            val = mine * e0[:, b:b + 1] + y_acc[rows, :] * e1[:, b:b + 1]
            att[core, rows, :] = val.astype(BF16).astype(F32)
        block = att.at[core, pl.ds(i * height, height)]
        copy = remote(block, block, g_send.at[i], g_recv.at[i], {'sp': partner})
        copy.start()
        g_copies.append(copy)
    for i in range(blocks):
        g_copies[i].wait_recv()
    for g in range(2):
        for j in range(group):
            n = g * group + j
            a_ref[:, n * HD:(n + 1) * HD] = att[g, pl.ds(j, seqs, stride=group), :].astype(BF16)
    w_copy.wait()

    chunks = part.shape[0]
    wide = part.shape[2]

    def compute(j):
        part[j] = jnp.dot(a_ref[...], w_buf[:, j * wide:(j + 1) * wide], preferred_element_type=F32)

    def emit(half, side, i, ref):
        at = (pl.ds(pl.multiple_of(half * seqs, seqs), seqs), pl.ds(pl.multiple_of(side * width + i * wide, wide), wide))
        out_ref[at] = (h_ref[at].astype(F32) + ref[i]).astype(BF16)

    def e_copy(i):
        return remote(part.at[i], e_buf.at[i], e_send.at[i], e_recv.at[i], {'tp': hub_of_end})

    def b_copy(i):
        return remote(a_buf.at[i], b_buf.at[i], b_send.at[i], b_recv.at[i], {'tp': other_hub})

    def t_copy(i):
        return remote(tot.at[i], tot.at[i], t_send.at[i], t_recv.at[i], {'tp': end_of_hub})

    def y_copy(i):
        return remote(tot.at[i], y_buf.at[i], ys.at[i], yr.at[i], {'sp': cross})

    def p1_copy(i):
        return remote(tot.at[i], p1_buf.at[i], p1s.at[i], p1r.at[i], {'sp': partner})

    def p2_copy(i):
        return remote(y_buf.at[i], p2_buf.at[i], p2s.at[i], p2r.at[i], {'sp': partner})

    def spread(i):
        y_copy(i).start()
        p1_copy(i).start()
        emit(y, core, i, tot)

    def pass_on(i):
        y_copy(i).wait_recv()
        p2_copy(i).start()
        emit(1 - y, core, i, y_buf)

    @pl.when(is_hub)
    def _():
        lag, lag2 = 3, 7
        for j in range(chunks):
            compute(j)
        for t in range(chunks + lag2):
            if t < chunks:
                e_copy(t).wait_recv()
                a_buf[t] = part[t] + e_buf[t]
                b_copy(t).start()
            i = t - lag
            if 0 <= i < chunks:
                b_copy(i).wait_recv()
                tot[i] = a_buf[i] + b_buf[i]
                t_copy(i).start()
                spread(i)
            i = t - lag2
            if 0 <= i < chunks:
                pass_on(i)
        for i in range(chunks):
            b_copy(i).wait_send()
            t_copy(i).wait_send()

    @pl.when(jnp.logical_not(is_hub))
    def _():
        lag = 4
        for j in range(chunks):
            compute(j)
            if j > 0:
                e_copy(j - 1).start()
        e_copy(chunks - 1).start()
        for t in range(chunks + lag):
            if t < chunks:
                t_copy(t).wait_recv()
                spread(t)
            i = t - lag
            if 0 <= i < chunks:
                pass_on(i)
        for i in range(chunks):
            e_copy(i).wait_send()

    for i in range(chunks):
        p1_copy(i).wait_recv()
        emit(y, other, i, p1_buf)
        p2_copy(i).wait_recv()
        emit(1 - y, other, i, p2_buf)
    for i in range(chunks):
        y_copy(i).wait_send()
        p1_copy(i).wait_send()
        p2_copy(i).wait_send()
    st_copy.wait_send()
    sy_copy.wait_send()
    for copy in d_copies + y_copies + g_copies:
        copy.wait_send()


def solution(mesh):
    cache_spec = P('dp', 'sp', 'tp', None)
    hbm = pl.BlockSpec(memory_space=pltpu.HBM)
    vmem = pl.BlockSpec(memory_space=pltpu.VMEM)
    smem = pl.BlockSpec(memory_space=pltpu.SMEM)
    dma = pltpu.SemaphoreType.DMA

    def local_step(hidden, norm_scale, w_qkv, w_out, k_cache, v_cache, positions):
        n_seq, seq_local, kv_local, head_dim = k_cache.shape
        d = hidden.shape[1]
        rows = seq_local * kv_local
        heads = w_qkv.shape[1] // head_dim
        group = heads // kv_local - 2
        k_flat = k_cache.reshape(n_seq, rows, head_dim)
        v_flat = v_cache.reshape(n_seq, rows, head_dim)
        share = heads // 4
        in_hbm = [pltpu.with_memory_space_constraint(a, pltpu.HBM)
                  for a in (hidden, norm_scale.reshape(d // head_dim, head_dim), positions.reshape(1, n_seq), w_qkv, k_flat, v_flat)]
        cache_type = pltpu.VMEM((n_seq, rows, head_dim), BF16)
        table = pltpu.VMEM((n_seq, head_dim), F32)
        groups = [2, 2, share - 4]
        qkv, k_vmem, v_vmem = pl.pallas_call(
            qkv_kernel,
            out_shape=[pltpu.VMEM((4, share, n_seq, head_dim), F32), cache_type, cache_type],
            in_specs=[hbm] * 6,
            out_specs=[vmem, vmem, vmem],
            scratch_shapes=[
                pltpu.VMEM((n_seq, d), BF16), pltpu.VMEM((d // head_dim, head_dim), BF16), pltpu.VMEM((1, n_seq), jnp.int32),
                *[pltpu.VMEM((d, n * head_dim), BF16) for n in groups], pltpu.VMEM((n_seq, d), BF16), table, table,
                dma((3,)), dma((3, 2)), dma((2,)), *[dma((3,)) for _ in range(6)],
            ],
            compiler_params=pltpu.CompilerParams(collective_id=0, has_side_effects=True, vmem_limit_bytes=24 << 20),
            name='qkv',
        )(*in_hbm)
        qkv = qkv.reshape(heads, n_seq, head_dim)

        batch = 8
        k_out, v_out, acc, stat = pl.pallas_call(
            attention_kernel,
            out_shape=[
                jax.ShapeDtypeStruct(k_flat.shape, BF16), jax.ShapeDtypeStruct(v_flat.shape, BF16),
                pltpu.VMEM((2, n_seq, group, head_dim), F32), pltpu.VMEM((2, group, head_dim), F32),
            ],
            in_specs=[smem, vmem, vmem, vmem],
            out_specs=[hbm, hbm, vmem, vmem],
            scratch_shapes=[
                pltpu.VMEM((n_seq * 2 * group, head_dim), F32), pltpu.VMEM((batch * 2 * group, rows), F32),
                pltpu.VMEM((batch * 2 * group, rows), BF16), dma((2, 8)),
            ],
            compiler_params=pltpu.CompilerParams(vmem_limit_bytes=16 << 20),
            name='attention',
        )(positions, qkv, k_vmem, v_vmem)
        acc = acc.reshape(2, n_seq * group, head_dim)

        width = d // 2
        depth = w_out.shape[0]
        wide = 2 * CHUNK
        chunks = width // wide
        blocks = 2
        seqs = n_seq // 2
        slot = pltpu.VMEM((chunks, seqs, wide), F32)
        whole = pltpu.VMEM((n_seq * group, head_dim), F32)
        half = pltpu.VMEM((seqs * group, head_dim), F32)
        tile = pltpu.VMEM((group, head_dim), F32)
        h_out = pl.pallas_call(
            project_kernel,
            out_shape=jax.ShapeDtypeStruct((n_seq, d), BF16),
            in_specs=[vmem, vmem, vmem, hbm],
            out_specs=vmem,
            scratch_shapes=[
                pltpu.VMEM((depth, width), BF16), whole, tile, whole, tile, half, tile,
                pltpu.VMEM((2, seqs * group, head_dim), F32), pltpu.VMEM((seqs, depth), BF16),
                slot, slot, slot, slot, slot, slot, slot, slot,
                dma(()), dma((2,)), dma((2,)), dma((2 * blocks,)), dma((2 * blocks,)), *[dma((blocks,)) for _ in range(4)],
                *[dma((chunks,)) for _ in range(12)],
            ],
            compiler_params=pltpu.CompilerParams(collective_id=1, has_side_effects=True, vmem_limit_bytes=40 << 20),
            name='project',
        )(hidden, acc, stat, pltpu.with_memory_space_constraint(w_out, pltpu.HBM))
        return h_out, k_out.reshape(k_cache.shape), v_out.reshape(v_cache.shape)

    return jax.shard_map(
        local_step,
        mesh=mesh,
        in_specs=(P('dp', None), P(None), P(None, 'tp'), P('tp', None), cache_spec, cache_spec, P('dp')),
        out_specs=(P('dp', None), cache_spec, cache_spec),
        check_vma=False,
    )
```

time: 77.7 us -> 61 us (0.79)
  Pallas kernels: 72.8 us -> 59.2 us
  local copies, waits for them, and re-layouts: 2.94 us -> 0.98 us
  other arithmetic: 0.95 us -> 0 us
    pallas_call x1, Pallas kernels: 19.3 us -> 7.32 us  [local_step(): pl.pallas_call(attention_kernel, out_shape=[jax.ShapeDtypeStruct(k_flat.s...]
    pallas_call x1, Pallas kernels: 40.6 us -> 36.6 us  [local_step(): pl.pallas_call(project_kernel, out_shape=jax.ShapeDtypeStruct((n_seq, d),...]
    pallas_call x1, Pallas kernels: 12.9 us -> 15.2 us  [local_step(): pl.pallas_call(qkv_kernel, out_shape=[pltpu.VMEM((4, share, n_seq, head_d...]
    unnamed x7 -> x5, local copies, waits for them, and re-layouts: 2.2 us -> 0.98 us
where the time goes in v2:
time: 61 us; the launch traced here: 60.9 us
  Pallas kernels  59.2 us (97%)
  local copies, waits for them, and re-layouts  0.98 us (2%)
  between operations  0.69 us (1%)
    pallas_call x1, Pallas kernels, local_step(): pl.pallas_call(project_kernel, out_shape=jax.ShapeDtypeStruct((n_seq, d),...  36.6 us
    pallas_call x1, Pallas kernels, local_step(): pl.pallas_call(qkv_kernel, out_shape=[pltpu.VMEM((4, share, n_seq, head_d...  15.2 us
    pallas_call x1, Pallas kernels, local_step(): pl.pallas_call(attention_kernel, out_shape=[jax.ShapeDtypeStruct(k_flat.s...  7.32 us

profile of v2, /device:TPU:0, one launch (start us, length us, event | category | flops | bytes accessed | tf_op | source)
XLA Modules:
  0.0 60.9 jit_solution(15782661164264327867)
XLA Ops:
  0.6 0.0 copy-start.1
  0.6 15.2 %qkv.1 = (f32[4,5,64,128]{3,2,1,0:T(8,128)S(1)}, bf16[64,512,128]{2,1,0:T(8,128)(2,1)S(1)}, bf16[64,512,128]{2,1,0:T(8,128)(2,1)S(1)}) custom-call(bf16[64,8192]{1,0:T(8,128)(2,1)} %h_ref.1, bf16[64,128]{1,0:T(8,128)(2,1)} %bitcast.13, s32[1,64]{1,0:T(1,128)} %bitcast.10, bf16[8192,2560]{1,0:T(8,128)(2,1)} %w_hbm.2, bf16[64,512,128]{2,1,0:T(8,128)(2,1)} %bitcast.11, ...), custom_call_target="tpu_custom_call" | custom-call | tf_op jit(solution)/shard_map/qkv/pallas_call | solution.py:459
  15.9 0.0 copy-done.1
  15.9 0.0 copy-start
  15.9 7.3 %attention.1 = (bf16[64,512,128]{2,1,0:T(8,128)(2,1)}, bf16[64,512,128]{2,1,0:T(8,128)(2,1)}, f32[2,64,8,128]{3,2,1,0:T(8,128)S(1)}, f32[2,8,128]{2,1,0:T(8,128)S(1)}) custom-call(s32[64]{0:T(128)S(1)} %copy-done.1, f32[20,64,128]{2,1,0:T(8,128)S(1)} %bitcast.8, bf16[64,512,128]{2,1,0:T(8,128)(2,1)S(1)} %get-tuple-element.11.k_ref, ...), custom_call_target="tpu_custom_call" | custom-call | tf_op jit(solution)/shard_map/attention/pallas_call | solution.py:475
  23.2 0.0 copy-done
  23.2 36.6 %project.1 = bf16[64,8192]{1,0:T(8,128)(2,1)S(1)} custom-call(bf16[64,8192]{1,0:T(8,128)(2,1)S(1)} %copy-done, f32[2,512,128]{2,1,0:T(8,128)S(1)} %bitcast.9, f32[2,8,128]{2,1,0:T(8,128)S(1)} %get-tuple-element.14.stat_ref, bf16[2048,8192]{1,0:T(8,128)(2,1)} %w_hbm.3), custom_call_target="tpu_custom_call" | custom-call | tf_op jit(solution)/shard_map/project/pallas_call | solution.py:502
  59.9 1.0 %copy.11 = bf16[64,8192]{1,0:T(8,128)(2,1)} copy(bf16[64,8192]{1,0:T(8,128)(2,1)S(1)} %project.1) | data formatting | bytes 2097152
Async XLA Ops:
  0.6 15.2 %copy-start.1 = (s32[64]{0:T(128)S(1)}, s32[64]{0:T(128)}, u32[]{:S(2)}) copy-start(s32[64]{0:T(128)} %pos_ref.1) | copy-start | bytes 772
  15.9 7.3 %copy-start = (bf16[64,8192]{1,0:T(8,128)(2,1)S(1)}, bf16[64,8192]{1,0:T(8,128)(2,1)}, u32[]{:S(2)}) copy-start(bf16[64,8192]{1,0:T(8,128)(2,1)} %h_ref.1) | copy-start | bytes 3145732

commit v3 on v2

--- a/solution.py
+++ b/solution.py
@@ -50,13 +50,13 @@
     for g, buf in enumerate(bufs):
         col = pl.multiple_of(sp * width + first, HD)
         first += buf.shape[1]
-        group = []
-        for i in range(pieces):
-            rows = pl.ds(i * depth, depth)
-            copy = pltpu.make_async_copy(w_hbm.at[rows, pl.ds(col, buf.shape[1])], buf.at[rows], w_sem.at[g, i])
-            copy.start()
-            group.append(copy)
-        w_copies.append(group)
+
+        def w_copy(i, g=g, buf=buf, col=col):
+            rows = pl.ds(pl.multiple_of(i * depth, depth), depth)
+            return pltpu.make_async_copy(w_hbm.at[rows, pl.ds(col, buf.shape[1])], buf.at[rows], w_sem.at[g, i])
+
+        lax.fori_loop(0, pieces, lambda i, carry, w_copy=w_copy: (w_copy(i).start(), carry)[1], 0)
+        w_copies.append([w_copy(i) for i in range(pieces)])
     enter([{'sp': partner}, {'sp': cross}])
 
     ins[0].wait()
@@ -100,10 +100,10 @@
         for i in range(pieces):
             w_copies[g][i].wait()
             rows = slice(i * depth, (i + 1) * depth)
+            if g >= 1 and i == 0:
+                cache_copies[g - 1].start()
             part = jnp.dot(u_ref[:, rows], buf[rows, :], preferred_element_type=F32)
             acc = part if acc is None else acc + part
-        if g >= 1:
-            cache_copies[g - 1].start()
         proj = jnp.clip(acc.astype(BF16).astype(F32), -8.0, 8.0)
         n = buf.shape[1] // HD
         for r in range(n):
@@ -157,18 +157,25 @@
                 ref[b, pl.ds(start, tile), :] = block.astype(BF16)
         return carry
 
-    lax.fori_loop(0, n_seq // at_once, patch, 0)
-    pieces = out_sem.shape[1]
-    span = n_seq // pieces
-    copies = []
-    for i in range(pieces):
-        for s, (src, dst) in enumerate(((k_ref, k_out), (v_ref, v_out))):
-            copy = pltpu.make_async_copy(src.at[pl.ds(i * span, span)], dst.at[pl.ds(i * span, span)], out_sem.at[s, i])
+    def out_copies(i):
+        span = pl.ds(i * at_once, at_once)
+        return [pltpu.make_async_copy(src.at[span], dst.at[span], out_sem.at[n, i])
+                for n, (src, dst) in enumerate(((k_ref, k_out), (v_ref, v_out)))]
+
+    def patch_and_write(i, carry):
+        patch(i, carry)
+        for copy in out_copies(i - 1):
             copy.start()
-            copies.append(copy)
+        return carry
+
+    pieces = n_seq // at_once
+    patch(0, 0)
+    lax.fori_loop(1, pieces, patch_and_write, 0)
     for g in range(2):
         for j in range(group):
             q_ref[pl.ds(g * group + j, n_seq, stride=n_q), :] = qkv_ref[g * per_kv + j]
+    for copy in out_copies(pieces - 1):
+        copy.start()
 
     col_id = lax.broadcasted_iota(jnp.int32, (n_q, rows), 1)
     head_id = lax.broadcasted_iota(jnp.int32, (n_q, rows), 0) // group
@@ -230,8 +237,9 @@
     weigh(steps - 1)
     stat_ref[0] = stats[:group]
     stat_ref[1] = stats[group:]
-    for copy in copies:
-        copy.wait()
+    for i in range(pieces):
+        for copy in out_copies(i):
+            copy.wait()
 
 
 def project_kernel(h_ref, acc_ref, stat_ref, w_hbm, out_ref, w_buf, d_acc, d_stat, m_acc, m_stat, y_acc, y_stat, att, a_ref,
@@ -344,8 +352,12 @@
     chunks = part.shape[0]
     wide = part.shape[2]
 
+    per_dot = 256 // wide
+
     def compute(j):
-        part[j] = jnp.dot(a_ref[...], w_buf[:, j * wide:(j + 1) * wide], preferred_element_type=F32)
+        val = jnp.dot(a_ref[...], w_buf[:, j * 256:(j + 1) * 256], preferred_element_type=F32)
+        for n in range(per_dot):
+            part[j * per_dot + n] = val[:, n * wide:(n + 1) * wide]
 
     def emit(half, side, i, ref):
         at = (pl.ds(pl.multiple_of(half * seqs, seqs), seqs), pl.ds(pl.multiple_of(side * width + i * wide, wide), wide))
@@ -381,8 +393,8 @@
 
     @pl.when(is_hub)
     def _():
-        lag, lag2 = 3, 7
-        for j in range(chunks):
+        lag, lag2 = 7, 15
+        for j in range(chunks // per_dot):
             compute(j)
         for t in range(chunks + lag2):
             if t < chunks:
@@ -404,12 +416,13 @@
 
     @pl.when(jnp.logical_not(is_hub))
     def _():
-        lag = 4
-        for j in range(chunks):
-            compute(j)
-            if j > 0:
-                e_copy(j - 1).start()
-        e_copy(chunks - 1).start()
+        lag = 8
+        for j in range(chunks // per_dot + 1):
+            if j < chunks // per_dot:
+                compute(j)
+            for n in range(per_dot):
+                if j > 0:
+                    e_copy((j - 1) * per_dot + n).start()
         for t in range(chunks + lag):
             if t < chunks:
                 t_copy(t).wait_recv()
@@ -491,9 +504,9 @@
 
         width = d // 2
         depth = w_out.shape[0]
-        wide = 2 * CHUNK
+        wide = CHUNK
         chunks = width // wide
-        blocks = 2
+        blocks = 4
         seqs = n_seq // 2
         slot = pltpu.VMEM((chunks, seqs, wide), F32)
         whole = pltpu.VMEM((n_seq * group, head_dim), F32)

time: 61 us -> 58.1 us (0.952)
  Pallas kernels: 59.2 us -> 56.3 us
    pallas_call x1, Pallas kernels: 15.2 us -> 12.5 us  [local_step(): pl.pallas_call(qkv_kernel, out_shape=[pltpu.VMEM((4, share, n_seq, head_d...]
    pallas_call x1, Pallas kernels: 7.32 us -> 6.66 us  [local_step(): pl.pallas_call(attention_kernel, out_shape=[jax.ShapeDtypeStruct(k_flat.s...]
where the time goes in v3:
time: 58.1 us; the launch traced here: 57.9 us
  Pallas kernels  56.3 us (97%)
  local copies, waits for them, and re-layouts  0.98 us (2%)
  between operations  0.69 us (1%)
    pallas_call x1, Pallas kernels, local_step(): pl.pallas_call(project_kernel, out_shape=jax.ShapeDtypeStruct((n_seq, d),...  37.1 us
    pallas_call x1, Pallas kernels, local_step(): pl.pallas_call(qkv_kernel, out_shape=[pltpu.VMEM((4, share, n_seq, head_d...  12.5 us
    pallas_call x1, Pallas kernels, local_step(): pl.pallas_call(attention_kernel, out_shape=[jax.ShapeDtypeStruct(k_flat.s...  6.66 us

profile of v3, /device:TPU:0, one launch (start us, length us, event | category | flops | bytes accessed | tf_op | source)
XLA Modules:
  0.0 57.9 jit_solution(7643475327766001118)
XLA Ops:
  0.6 0.0 copy-start.1
  0.6 12.5 %qkv.1 = (f32[4,5,64,128]{3,2,1,0:T(8,128)S(1)}, bf16[64,512,128]{2,1,0:T(8,128)(2,1)S(1)}, bf16[64,512,128]{2,1,0:T(8,128)(2,1)S(1)}) custom-call(bf16[64,8192]{1,0:T(8,128)(2,1)} %h_ref.1, bf16[64,128]{1,0:T(8,128)(2,1)} %bitcast.13, s32[1,64]{1,0:T(1,128)} %bitcast.10, bf16[8192,2560]{1,0:T(8,128)(2,1)} %w_hbm.2, bf16[64,512,128]{2,1,0:T(8,128)(2,1)} %bitcast.11, ...), custom_call_target="tpu_custom_call" | custom-call | tf_op jit(solution)/shard_map/qkv/pallas_call | solution.py:472
  13.2 0.0 copy-done.1
  13.2 0.0 copy-start
  13.2 6.7 %attention.1 = (bf16[64,512,128]{2,1,0:T(8,128)(2,1)}, bf16[64,512,128]{2,1,0:T(8,128)(2,1)}, f32[2,64,8,128]{3,2,1,0:T(8,128)S(1)}, f32[2,8,128]{2,1,0:T(8,128)S(1)}) custom-call(s32[64]{0:T(128)S(1)} %copy-done.1, f32[20,64,128]{2,1,0:T(8,128)S(1)} %bitcast.8, bf16[64,512,128]{2,1,0:T(8,128)(2,1)S(1)} %get-tuple-element.11.k_ref, ...), custom_call_target="tpu_custom_call" | custom-call | tf_op jit(solution)/shard_map/attention/pallas_call | solution.py:488
  19.9 0.0 copy-done
  19.9 37.1 %project.1 = bf16[64,8192]{1,0:T(8,128)(2,1)S(1)} custom-call(bf16[64,8192]{1,0:T(8,128)(2,1)S(1)} %copy-done, f32[2,512,128]{2,1,0:T(8,128)S(1)} %bitcast.9, f32[2,8,128]{2,1,0:T(8,128)S(1)} %get-tuple-element.14.stat_ref, bf16[2048,8192]{1,0:T(8,128)(2,1)} %w_hbm.3), custom_call_target="tpu_custom_call" | custom-call | tf_op jit(solution)/shard_map/project/pallas_call | solution.py:515
  57.0 1.0 %copy.11 = bf16[64,8192]{1,0:T(8,128)(2,1)} copy(bf16[64,8192]{1,0:T(8,128)(2,1)S(1)} %project.1) | data formatting | bytes 2097152
Async XLA Ops:
  0.6 12.5 %copy-start.1 = (s32[64]{0:T(128)S(1)}, s32[64]{0:T(128)}, u32[]{:S(2)}) copy-start(s32[64]{0:T(128)} %pos_ref.1) | copy-start | bytes 772
  13.2 6.7 %copy-start = (bf16[64,8192]{1,0:T(8,128)(2,1)S(1)}, bf16[64,8192]{1,0:T(8,128)(2,1)}, u32[]{:S(2)}) copy-start(bf16[64,8192]{1,0:T(8,128)(2,1)} %h_ref.1) | copy-start | bytes 3145732

commit v4 on v3

--- a/solution.py
+++ b/solution.py
@@ -131,13 +131,12 @@
         forward[g].wait()
 
 
-def attention_kernel(pos_ref, qkv_ref, k_ref, v_ref, k_out, v_out, acc_ref, stat_ref, q_ref, s_ref, p_ref, out_sem):
+def prepare_kernel(pos_ref, qkv_ref, k_ref, v_ref, q_ref, k_new, v_new):
     n_seq, rows, _ = k_ref.shape
-    seq_local = rows // 2
-    group = acc_ref.shape[2]
-    base = lax.axis_index('sp') * seq_local
+    base = lax.axis_index('sp') * (rows // 2)
+    n_q = q_ref.shape[0] // n_seq
+    group = n_q // 2
     per_kv = group + 2
-    n_q = 2 * group
 
     tile = 16
     row_id = lax.broadcasted_iota(jnp.int32, (tile, HD), 0)
@@ -149,105 +148,41 @@
             row = 2 * (pos_ref[b] - base)
             start = pl.multiple_of(jnp.clip(row // tile, 0, rows // tile - 1) * tile, tile)
             off = row - start
-            for ref, slot in ((k_ref, group), (v_ref, group + 1)):
+            for ref, new, slot in ((k_ref, k_new, group), (v_ref, v_new, group + 1)):
                 block = ref[b, pl.ds(start, tile), :].astype(F32)
                 one = qkv_ref[slot, pl.ds(b, 1), :]
                 two = qkv_ref[per_kv + slot, pl.ds(b, 1), :]
                 block = jnp.where(row_id == off, one, jnp.where(row_id == off + 1, two, block))
-                ref[b, pl.ds(start, tile), :] = block.astype(BF16)
+                new[b, pl.ds(start, tile), :] = block.astype(BF16)
         return carry
 
-    def out_copies(i):
-        span = pl.ds(i * at_once, at_once)
-        return [pltpu.make_async_copy(src.at[span], dst.at[span], out_sem.at[n, i])
-                for n, (src, dst) in enumerate(((k_ref, k_out), (v_ref, v_out)))]
-
-    def patch_and_write(i, carry):
-        patch(i, carry)
-        for copy in out_copies(i - 1):
-            copy.start()
-        return carry
-
-    pieces = n_seq // at_once
-    patch(0, 0)
-    lax.fori_loop(1, pieces, patch_and_write, 0)
+    lax.fori_loop(0, n_seq // at_once, patch, 0)
     for g in range(2):
         for j in range(group):
             q_ref[pl.ds(g * group + j, n_seq, stride=n_q), :] = qkv_ref[g * per_kv + j]
-    for copy in out_copies(pieces - 1):
+
+
+def finish_kernel(h_ref, k_ref, v_ref, h_out, k_out, v_out, h_sem, out_sem):
+    pieces = out_sem.shape[1]
+    span = k_ref.shape[0] // pieces
+    copies = [pltpu.make_async_copy(h_ref, h_out, h_sem)]
+    for i in range(pieces):
+        for n, (src, dst) in enumerate(((k_ref, k_out), (v_ref, v_out))):
+            at = pl.ds(i * span, span)
+            copies.append(pltpu.make_async_copy(src.at[at], dst.at[at], out_sem.at[n, i]))
+    for copy in copies:
         copy.start()
-
-    col_id = lax.broadcasted_iota(jnp.int32, (n_q, rows), 1)
-    head_id = lax.broadcasted_iota(jnp.int32, (n_q, rows), 0) // group
-    col_key = jnp.where(lax.rem(col_id, 2) == head_id, col_id, 1 << 30)
-    lane = lax.broadcasted_iota(jnp.int32, (n_q, HD), 1)
-    upper = lax.broadcasted_iota(jnp.int32, (2 * n_q, HD), 0) < n_q
-    factor = HD ** -0.5 * math.log2(math.e)
-    pairs = s_ref.shape[0] // (2 * n_q)
-    batch = 2 * pairs
-
-    def score(i):
-        for r in range(pairs):
-            b = i * batch + 2 * r
-            q = q_ref[pl.ds(pl.multiple_of(b * n_q, 2 * n_q), 2 * n_q), :]
-            lhs = jnp.concatenate([jnp.where(upper, q, 0.0), jnp.where(upper, 0.0, q)], axis=1).astype(BF16)
-            rhs = jnp.concatenate([k_ref[b], k_ref[b + 1]], axis=1)
-            out = lax.dot_general(lhs, rhs, (((1,), (1,)), ((), ())), preferred_element_type=F32)
-            for e in range(2):
-                limit = 2 * (pos_ref[b + e] - base + 1)
-                half = out[e * n_q:(e + 1) * n_q] * factor
-                s_ref[(2 * r + e) * n_q:(2 * r + e + 1) * n_q, :] = jnp.where(col_key < limit, half, NEG)
-
-    def soften(i, stats):
-        for r in range(batch):
-            b = i * batch + r
-            scores = s_ref[r * n_q:(r + 1) * n_q, :]
-            top = jnp.maximum(jnp.max(scores, axis=-1, keepdims=True), FLOOR)
-            probs = jnp.exp2(scores - top)
-            total = jnp.sum(probs, axis=-1, keepdims=True)
-            p_ref[r * n_q:(r + 1) * n_q, :] = probs.astype(BF16)
-            stats = jnp.where(lane == b, top, jnp.where(lane == b + n_seq, total, stats))
-        return stats
-
-    def weigh(i):
-        for r in range(pairs):
-            b = i * batch + 2 * r
-            rhs = jnp.concatenate([v_ref[b], v_ref[b + 1]], axis=1)
-            out = jnp.dot(p_ref[2 * r * n_q:(2 * r + 2) * n_q, :], rhs, preferred_element_type=F32)
-            for e in range(2):
-                own = out[e * n_q:(e + 1) * n_q, e * HD:(e + 1) * HD]
-                acc_ref[0, b + e] = own[:group]
-                acc_ref[1, b + e] = own[group:]
-
-    steps = n_seq // batch
-    stats = jnp.zeros((n_q, HD), F32)
-    score(0)
-    stats = soften(0, stats)
-    score(1)
-
-    def step(i, stats):
-        weigh(i)
-        stats = soften(i + 1, stats)
-        score(i + 2)
-        return stats
-
-    stats = lax.fori_loop(0, steps - 2, step, stats)
-    weigh(steps - 2)
-    stats = soften(steps - 1, stats)
-    weigh(steps - 1)
-    stat_ref[0] = stats[:group]
-    stat_ref[1] = stats[group:]
-    for i in range(pieces):
-        for copy in out_copies(i):
-            copy.wait()
-
-
-def project_kernel(h_ref, acc_ref, stat_ref, w_hbm, out_ref, w_buf, d_acc, d_stat, m_acc, m_stat, y_acc, y_stat, att, a_ref,
+    for copy in copies:
+        copy.wait()
+
+
+def project_kernel(pos_ref, q_ref, k_ref, v_ref, h_ref, w_hbm, out_ref, w_buf, s_ref, p_ref, acc, d_acc, m_acc, y_acc, att, a_ref,
                    part, e_buf, a_buf, b_buf, tot, y_buf, p1_buf, p2_buf,
-                   w_sem, st_send, st_recv, d_send, d_recv, y_send, y_recv, g_send, g_recv,
+                   w_sem, d_send, d_recv, y_send, y_recv, g_send, g_recv,
                    e_send, e_recv, b_send, b_recv, t_send, t_recv, ys, yr, p1s, p1r, p2s, p2r):
     sp, partner, cross = sp_peers()
     core = lax.rem(sp, 2)
+    other = 1 - core
     y = sp // 2
     z = lax.axis_index('tp')
     is_hub = (z == 1) | (z == 2)
@@ -267,33 +202,69 @@
     def _():
         for peer in ({'tp': end_of_hub}, {'tp': other_hub}):
             pl.semaphore_signal(barrier, inc=1, device_id=peer, device_id_type=MESH_ID)
-        pl.semaphore_wait(barrier, 4)
 
     @pl.when(jnp.logical_not(is_hub))
     def _():
         pl.semaphore_signal(barrier, inc=1, device_id={'tp': hub_of_end}, device_id_type=MESH_ID)
-        pl.semaphore_wait(barrier, 3)
-
-    group = stat_ref.shape[1]
-    seqs = out_ref.shape[0] // 2
-    blocks = y_send.shape[0]
-    span = seqs // blocks
+
+    n_seq, rows, _ = k_ref.shape
+    n_q = q_ref.shape[0] // n_seq
+    group = n_q // 2
+    seqs = n_seq // 2
+    units = acc.shape[0]
+    span = n_seq // units
     height = span * group
-    other = 1 - core
-    st_copy = remote(stat_ref.at[other], d_stat, st_send.at[0], st_recv.at[0], {'sp': partner})
-    st_copy.start()
-
-    def rows_of(half, i):
-        return pl.ds(pl.multiple_of((half * blocks + i) * height, height), height)
-
-    d_copies = []
-    for n in range(2 * blocks):
-        rows = rows_of(1 - y if n < blocks else y, n % blocks)
-        copy = remote(acc_ref.at[other, rows], d_acc.at[rows], d_send.at[n], d_recv.at[n], {'sp': partner})
-        copy.start()
-        d_copies.append(copy)
-    st_copy.wait_recv()
-    lane = lax.broadcasted_iota(jnp.int32, (group, HD), 1)
+    base = sp * (rows // 2)
+    firsts = [(1 - y) * seqs, (1 - y) * seqs + span, y * seqs, y * seqs + span]
+    col_id = lax.broadcasted_iota(jnp.int32, (n_q, rows), 1)
+    head_id = lax.broadcasted_iota(jnp.int32, (n_q, rows), 0) // group
+    col_key = jnp.where(lax.rem(col_id, 2) == head_id, col_id, 1 << 30)
+    lane = lax.broadcasted_iota(jnp.int32, (n_q, HD), 1)
+    low = lax.broadcasted_iota(jnp.int32, (group, HD), 1) < HD // 2
+    upper = lax.broadcasted_iota(jnp.int32, (2 * n_q, HD), 0) < n_q
+    factor = HD ** -0.5 * math.log2(math.e)
+    batch = s_ref.shape[0] // n_q
+    per_unit = span // batch
+    steps = units * per_unit
+    stats = [jnp.zeros((n_q, HD), F32) for _ in range(units)]
+
+    def score(i):
+        for r in range(0, batch, 2):
+            b = firsts[i // per_unit] + (i % per_unit) * batch + r
+            q = q_ref[pl.ds(pl.multiple_of(b * n_q, 2 * n_q), 2 * n_q), :]
+            lhs = jnp.concatenate([jnp.where(upper, q, 0.0), jnp.where(upper, 0.0, q)], axis=1).astype(BF16)
+            rhs = jnp.concatenate([k_ref[b], k_ref[b + 1]], axis=1)
+            out = lax.dot_general(lhs, rhs, (((1,), (1,)), ((), ())), preferred_element_type=F32)
+            for e in range(2):
+                limit = 2 * (pos_ref[b + e] - base + 1)
+                half = out[e * n_q:(e + 1) * n_q] * factor
+                s_ref[(r + e) * n_q:(r + e + 1) * n_q, :] = jnp.where(col_key < limit, half, NEG)
+
+    def soften(i):
+        u = i // per_unit
+        for r in range(batch):
+            at = (i % per_unit) * batch + r
+            scores = s_ref[r * n_q:(r + 1) * n_q, :]
+            top = jnp.maximum(jnp.max(scores, axis=-1, keepdims=True), FLOOR)
+            probs = jnp.exp2(scores - top)
+            total = jnp.sum(probs, axis=-1, keepdims=True)
+            p_ref[r * n_q:(r + 1) * n_q, :] = probs.astype(BF16)
+            stats[u] = jnp.where(lane == at, top, jnp.where(lane == at + HD // 2, total, stats[u]))
+
+    def weigh(i):
+        u = i // per_unit
+        for r in range(0, batch, 2):
+            at = (i % per_unit) * batch + r
+            b = firsts[u] + at
+            rhs = jnp.concatenate([v_ref[b], v_ref[b + 1]], axis=1)
+            out = jnp.dot(p_ref[r * n_q:(r + 2) * n_q, :], rhs, preferred_element_type=F32)
+            for e in range(2):
+                own = out[e * n_q:(e + 1) * n_q, e * HD:(e + 1) * HD]
+                acc[u, 0, (at + e) * group:(at + e + 1) * group, :] = own[:group]
+                acc[u, 1, (at + e) * group:(at + e + 1) * group, :] = own[group:]
+        if i % per_unit == per_unit - 1:
+            acc[u, 0, height:, :] = stats[u][:group]
+            acc[u, 1, height:, :] = stats[u][group:]
 
     def weights(s0, s1):
         l0, l1 = pltpu.roll(s0, HD // 2, 1), pltpu.roll(s1, HD // 2, 1)
@@ -301,48 +272,64 @@
         e0, e1 = jnp.exp2(s0 - top), jnp.exp2(s1 - top)
         return top, e0, e1, l0 * e0 + l1 * e1
 
-    def lanes_of(half, val):
-        return jnp.where(half == 0, val, pltpu.roll(val, HD - seqs, 1))
-
-    top, e0, e1, total = weights(stat_ref[core], d_stat[...])
-    m_stat[...] = jnp.where(lane < HD // 2, top, pltpu.roll(total, HD // 2, 1))
-    sy_copy = remote(m_stat, y_stat, st_send.at[1], st_recv.at[1], {'sp': cross})
-    y_copies = []
-    for n in range(2 * blocks):
-        half, i = (1 - y if n < blocks else y), n % blocks
-        d_copies[n].wait_recv()
-        f0, f1 = lanes_of(half, e0), lanes_of(half, e1)
-        first = half * seqs * group
+    def d_copy(u):
+        return remote(acc.at[u, other], d_acc.at[u], d_send.at[u], d_recv.at[u], {'sp': partner})
+
+    def m_copy(u):
+        return remote(m_acc.at[u], y_acc.at[u], y_send.at[u], y_recv.at[u], {'sp': cross})
+
+    def g_copy(u):
+        block = att.at[core, pl.ds(u * height, height)]
+        return remote(block, block, g_send.at[u], g_recv.at[u], {'sp': partner})
+
+    def merge(u):
+        d_copy(u).wait_recv()
+        top, e0, e1, total = weights(acc[u, core, height:, :], d_acc[u, height:, :])
+        m_acc[u, height:, :] = jnp.where(low, top, pltpu.roll(total, HD // 2, 1))
         for r in range(span):
-            b = i * span + r
-            rows = pl.ds(pl.multiple_of(first + b * group, group), group)
-            m_acc[rows, :] = acc_ref[core, rows, :] * f0[:, b:b + 1] + d_acc[rows, :] * f1[:, b:b + 1]
-        if n == 0:
-            sy_copy.start()
-        if n < blocks:
-            copy = remote(m_acc.at[rows_of(half, i)], y_acc.at[pl.ds(i * height, height)], y_send.at[i], y_recv.at[i], {'sp': cross})
-            copy.start()
-            y_copies.append(copy)
-    sy_copy.wait_recv()
-    top, e0, e1, total = weights(m_stat[...], y_stat[...])
-    share = 1.0 / jnp.where(lane < HD // 2, total, 1.0)
-    e0, e1 = lanes_of(y, e0 * share), lanes_of(y, e1 * share)
-    first = y * seqs * group
-    g_copies = []
-    for i in range(blocks):
-        y_copies[i].wait_recv()
+            at = slice(r * group, (r + 1) * group)
+            m_acc[u, at, :] = acc[u, core, at, :] * e0[:, r:r + 1] + d_acc[u, at, :] * e1[:, r:r + 1]
+        if u < units // 2:
+            m_copy(u).start()
+
+    def settle(u):
+        m_copy(u).wait_recv()
+        own = units // 2 + u
+        top, e0, e1, total = weights(m_acc[own, height:, :], y_acc[u, height:, :])
+        share = 1.0 / jnp.where(low, total, 1.0)
+        e0, e1 = e0 * share, e1 * share
         for r in range(span):
-            b = i * span + r
-            rows = pl.ds(b * group, group)
-            mine = m_acc[pl.ds(pl.multiple_of(first + b * group, group), group), :]
-            val = mine * e0[:, b:b + 1] + y_acc[rows, :] * e1[:, b:b + 1]
-            att[core, rows, :] = val.astype(BF16).astype(F32)
-        block = att.at[core, pl.ds(i * height, height)]
-        copy = remote(block, block, g_send.at[i], g_recv.at[i], {'sp': partner})
-        copy.start()
-        g_copies.append(copy)
-    for i in range(blocks):
-        g_copies[i].wait_recv()
+            at = slice(r * group, (r + 1) * group)
+            val = m_acc[own, at, :] * e0[:, r:r + 1] + y_acc[u, at, :] * e1[:, r:r + 1]
+            att[core, u * height + r * group:u * height + (r + 1) * group, :] = val.astype(BF16).astype(F32)
+        g_copy(u).start()
+
+    for i in range(-2, steps):
+        if i >= 0:
+            weigh(i)
+        if 0 <= i + 1 < steps:
+            soften(i + 1)
+        if i + 2 < steps:
+            score(i + 2)
+        if i >= 0 and i % per_unit == per_unit - 1:
+            u = i // per_unit
+            if u == 0:
+                @pl.when(is_hub)
+                def _():
+                    pl.semaphore_wait(barrier, 4)
+
+                @pl.when(jnp.logical_not(is_hub))
+                def _():
+                    pl.semaphore_wait(barrier, 3)
+
+            d_copy(u).start()
+            if u > 0:
+                merge(u - 1)
+    settle(0)
+    merge(units - 1)
+    settle(1)
+    for u in range(units // 2):
+        g_copy(u).wait_recv()
     for g in range(2):
         for j in range(group):
             n = g * group + j
@@ -442,10 +429,11 @@
         y_copy(i).wait_send()
         p1_copy(i).wait_send()
         p2_copy(i).wait_send()
-    st_copy.wait_send()
-    sy_copy.wait_send()
-    for copy in d_copies + y_copies + g_copies:
-        copy.wait_send()
+    for u in range(units):
+        d_copy(u).wait_send()
+    for u in range(units // 2):
+        m_copy(u).wait_send()
+        g_copy(u).wait_send()
 
 
 def solution(mesh):
@@ -484,49 +472,52 @@
         )(*in_hbm)
         qkv = qkv.reshape(heads, n_seq, head_dim)
 
-        batch = 8
-        k_out, v_out, acc, stat = pl.pallas_call(
-            attention_kernel,
-            out_shape=[
-                jax.ShapeDtypeStruct(k_flat.shape, BF16), jax.ShapeDtypeStruct(v_flat.shape, BF16),
-                pltpu.VMEM((2, n_seq, group, head_dim), F32), pltpu.VMEM((2, group, head_dim), F32),
-            ],
+        query, k_vmem, v_vmem = pl.pallas_call(
+            prepare_kernel,
+            out_shape=[pltpu.VMEM((n_seq * 2 * group, head_dim), F32), cache_type, cache_type],
             in_specs=[smem, vmem, vmem, vmem],
-            out_specs=[hbm, hbm, vmem, vmem],
-            scratch_shapes=[
-                pltpu.VMEM((n_seq * 2 * group, head_dim), F32), pltpu.VMEM((batch * 2 * group, rows), F32),
-                pltpu.VMEM((batch * 2 * group, rows), BF16), dma((2, 8)),
-            ],
-            compiler_params=pltpu.CompilerParams(vmem_limit_bytes=16 << 20),
-            name='attention',
+            out_specs=[vmem, vmem, vmem],
+            input_output_aliases={2: 1, 3: 2},
+            compiler_params=pltpu.CompilerParams(vmem_limit_bytes=8 << 20),
+            name='prepare',
         )(positions, qkv, k_vmem, v_vmem)
-        acc = acc.reshape(2, n_seq * group, head_dim)
 
         width = d // 2
         depth = w_out.shape[0]
         wide = CHUNK
         chunks = width // wide
-        blocks = 4
+        batch, units = 8, 4
         seqs = n_seq // 2
+        block = n_seq // units * group
         slot = pltpu.VMEM((chunks, seqs, wide), F32)
-        whole = pltpu.VMEM((n_seq * group, head_dim), F32)
-        half = pltpu.VMEM((seqs * group, head_dim), F32)
-        tile = pltpu.VMEM((group, head_dim), F32)
-        h_out = pl.pallas_call(
+        h_new = pl.pallas_call(
             project_kernel,
-            out_shape=jax.ShapeDtypeStruct((n_seq, d), BF16),
-            in_specs=[vmem, vmem, vmem, hbm],
+            out_shape=pltpu.VMEM((n_seq, d), BF16),
+            in_specs=[smem, vmem, vmem, vmem, vmem, hbm],
             out_specs=vmem,
             scratch_shapes=[
-                pltpu.VMEM((depth, width), BF16), whole, tile, whole, tile, half, tile,
+                pltpu.VMEM((depth, width), BF16),
+                pltpu.VMEM((batch * 2 * group, rows), F32), pltpu.VMEM((batch * 2 * group, rows), BF16),
+                pltpu.VMEM((units, 2, block + group, head_dim), F32), pltpu.VMEM((units, block + group, head_dim), F32),
+                pltpu.VMEM((units, block + group, head_dim), F32), pltpu.VMEM((units // 2, block + group, head_dim), F32),
                 pltpu.VMEM((2, seqs * group, head_dim), F32), pltpu.VMEM((seqs, depth), BF16),
                 slot, slot, slot, slot, slot, slot, slot, slot,
-                dma(()), dma((2,)), dma((2,)), dma((2 * blocks,)), dma((2 * blocks,)), *[dma((blocks,)) for _ in range(4)],
+                dma(()), dma((units,)), dma((units,)), *[dma((units // 2,)) for _ in range(4)],
                 *[dma((chunks,)) for _ in range(12)],
             ],
-            compiler_params=pltpu.CompilerParams(collective_id=1, has_side_effects=True, vmem_limit_bytes=40 << 20),
+            compiler_params=pltpu.CompilerParams(collective_id=1, has_side_effects=True, vmem_limit_bytes=30 << 20),
             name='project',
-        )(hidden, acc, stat, pltpu.with_memory_space_constraint(w_out, pltpu.HBM))
+        )(positions, query, k_vmem, v_vmem, hidden, pltpu.with_memory_space_constraint(w_out, pltpu.HBM))
+
+        h_out, k_out, v_out = pl.pallas_call(
+            finish_kernel,
+            out_shape=[jax.ShapeDtypeStruct(a.shape, BF16) for a in (hidden, k_flat, v_flat)],
+            in_specs=[vmem, vmem, vmem],
+            out_specs=[hbm, hbm, hbm],
+            scratch_shapes=[dma(()), dma((2, 8))],
+            compiler_params=pltpu.CompilerParams(vmem_limit_bytes=2 << 20),
+            name='finish',
+        )(h_new, k_vmem, v_vmem)
         return h_out, k_out.reshape(k_cache.shape), v_out.reshape(v_cache.shape)
 
     return jax.shard_map(

time: 58.1 us -> 59.7 us (1.028)
  Pallas kernels: 56.3 us -> 58.7 us
  local copies, waits for them, and re-layouts: 0.98 us -> 0.01 us
    pallas_call x2 -> x3, Pallas kernels: 43.7 us -> 46.2 us  [the longest x1 38.4 us: local_step(): pl.pallas_call(project_kernel, out_shape=pltpu.VMEM((n_seq, d), BF16), in...]
    unnamed x5 -> x4, local copies, waits for them, and re-layouts: 0.98 us -> 0.01 us
where the time goes in v4:
time: 59.7 us; the launch traced here: 59.5 us
  Pallas kernels  58.7 us (98%)
  between operations  0.85 us (1%)
    pallas_call x1, Pallas kernels, local_step(): pl.pallas_call(project_kernel, out_shape=pltpu.VMEM((n_seq, d), BF16), in...  38.4 us
    pallas_call x1, Pallas kernels, local_step(): pl.pallas_call(qkv_kernel, out_shape=[pltpu.VMEM((4, share, n_seq, head_d...  12.5 us
    pallas_call x1, Pallas kernels, local_step(): pl.pallas_call(finish_kernel, out_shape=[jax.ShapeDtypeStruct(a.shape, BF...  6.29 us
    pallas_call x1, Pallas kernels, local_step(): pl.pallas_call(prepare_kernel, out_shape=[pltpu.VMEM((n_seq * 2 * group,...  1.44 us

profile of v4, /device:TPU:0, one launch (start us, length us, event | category | flops | bytes accessed | tf_op | source)
XLA Modules:
  0.0 59.5 jit_solution(13475404453144232389)
XLA Ops:
  0.6 0.0 copy-start.1
  0.6 12.5 %qkv.1 = (f32[4,5,64,128]{3,2,1,0:T(8,128)S(1)}, bf16[64,512,128]{2,1,0:T(8,128)(2,1)S(1)}, bf16[64,512,128]{2,1,0:T(8,128)(2,1)S(1)}) custom-call(bf16[64,8192]{1,0:T(8,128)(2,1)} %h_ref.1, bf16[64,128]{1,0:T(8,128)(2,1)} %bitcast.11, s32[1,64]{1,0:T(1,128)} %bitcast.8, bf16[8192,2560]{1,0:T(8,128)(2,1)} %w_hbm.2, bf16[64,512,128]{2,1,0:T(8,128)(2,1)} %bitcast.9, ...), custom_call_target="tpu_custom_call" | custom-call | tf_op jit(solution)/shard_map/qkv/pallas_call | solution.py:460
  13.2 0.0 copy-done.1
  13.2 0.0 copy-start
  13.2 1.4 %prepare.1 = (f32[1024,128]{1,0:T(8,128)S(1)}, bf16[64,512,128]{2,1,0:T(8,128)(2,1)S(1)}, bf16[64,512,128]{2,1,0:T(8,128)(2,1)S(1)}) custom-call(s32[64]{0:T(128)S(1)} %copy-done.1, f32[20,64,128]{2,1,0:T(8,128)S(1)} %bitcast.7, bf16[64,512,128]{2,1,0:T(8,128)(2,1)S(1)} %get-tuple-element.13.k_ref, ...), custom_call_target="tpu_custom_call", output_to_operand_aliasing={{1}: (2, {}), {2}: (3, {})} | custom-call | tf_op jit(solution)/shard_map/prepare/pallas_call | solution.py:475
  14.6 0.0 copy-done
  14.6 38.4 %project.1.h_ref = bf16[64,8192]{1,0:T(8,128)(2,1)S(1)} custom-call(s32[64]{0:T(128)S(1)} %copy-done.1, f32[1024,128]{1,0:T(8,128)S(1)} %get-tuple-element.15.q_ref, bf16[64,512,128]{2,1,0:T(8,128)(2,1)S(1)} %get-tuple-element.16.k_ref, bf16[64,512,128]{2,1,0:T(8,128)(2,1)S(1)} %get-tuple-element.17.v_ref, bf16[64,8192]{1,0:T(8,128)(2,1)S(1)} %copy-done, ...), custom_call_target="tpu_custom_call" | custom-call | tf_op jit(solution)/shard_map/project/pallas_call | solution.py:493
  53.1 6.3 %finish.1 = (bf16[64,8192]{1,0:T(8,128)(2,1)}, bf16[64,512,128]{2,1,0:T(8,128)(2,1)}, bf16[64,512,128]{2,1,0:T(8,128)(2,1)}) custom-call(bf16[64,8192]{1,0:T(8,128)(2,1)S(1)} %project.1.h_ref, bf16[64,512,128]{2,1,0:T(8,128)(2,1)S(1)} %get-tuple-element.16.k_ref, bf16[64,512,128]{2,1,0:T(8,128)(2,1)S(1)} %get-tuple-element.17.v_ref), custom_call_target="tpu_custom_call" | custom-call | tf_op jit(solution)/shard_map/finish/pallas_call | solution.py:512
Async XLA Ops:
  0.6 12.5 %copy-start.1 = (s32[64]{0:T(128)S(1)}, s32[64]{0:T(128)}, u32[]{:S(2)}) copy-start(s32[64]{0:T(128)} %pos_ref.3) | copy-start | bytes 772
  13.2 1.5 %copy-start = (bf16[64,8192]{1,0:T(8,128)(2,1)S(1)}, bf16[64,8192]{1,0:T(8,128)(2,1)}, u32[]{:S(2)}) copy-start(bf16[64,8192]{1,0:T(8,128)(2,1)} %h_ref.1) | copy-start | bytes 3145732

commit v5 on v3

--- a/solution.py
+++ b/solution.py
@@ -1,3 +1,4 @@
+import functools
 import math
 import jax
 import jax.numpy as jnp
@@ -242,7 +243,7 @@
             copy.wait()
 
 
-def project_kernel(h_ref, acc_ref, stat_ref, w_hbm, out_ref, w_buf, d_acc, d_stat, m_acc, m_stat, y_acc, y_stat, att, a_ref,
+def project_kernel(split, h_ref, acc_ref, stat_ref, w_hbm, out_ref, w_buf, d_acc, d_stat, m_acc, m_stat, y_acc, y_stat, att, a_ref,
                    part, e_buf, a_buf, b_buf, tot, y_buf, p1_buf, p2_buf,
                    w_sem, st_send, st_recv, d_send, d_recv, y_send, y_recv, g_send, g_recv,
                    e_send, e_recv, b_send, b_recv, t_send, t_recv, ys, yr, p1s, p1r, p2s, p2r):
@@ -254,10 +255,19 @@
     end_of_hub = 3 * (z - 1)
     hub_of_end = 1 + z // 2
     other_hub = 3 - z
-    width = w_buf.shape[1]
-    col = pl.multiple_of(core * width, HD)
-    w_copy = pltpu.make_async_copy(w_hbm.at[:, pl.ds(col, width)], w_buf, w_sem)
-    w_copy.start()
+    few, many = split
+    wide = part.shape[2]
+
+    def on_side(side, then):
+        for c, n in ((0, few), (1, many)):
+            @pl.when(side == c)
+            def _(c=c, n=n):
+                then(c, n)
+
+    def w_copy(c, n):
+        return pltpu.make_async_copy(w_hbm.at[:, pl.ds(c * few * wide, n * wide)], w_buf.at[:, pl.ds(0, n * wide)], w_sem)
+
+    on_side(core, lambda c, n: w_copy(c, n).start())
 
     barrier = pltpu.get_barrier_semaphore()
     for peer in ({'sp': partner}, {'sp': cross}):
@@ -328,8 +338,11 @@
     share = 1.0 / jnp.where(lane < HD // 2, total, 1.0)
     e0, e1 = lanes_of(y, e0 * share), lanes_of(y, e1 * share)
     first = y * seqs * group
-    g_copies = []
-    for i in range(blocks):
+    def g_copy(i):
+        block = att.at[core, pl.ds(i * height, height)]
+        return remote(block, block, g_send.at[i], g_recv.at[i], {'sp': partner})
+
+    def settle(i):
         y_copies[i].wait_recv()
         for r in range(span):
             b = i * span + r
@@ -337,30 +350,38 @@
             mine = m_acc[pl.ds(pl.multiple_of(first + b * group, group), group), :]
             val = mine * e0[:, b:b + 1] + y_acc[rows, :] * e1[:, b:b + 1]
             att[core, rows, :] = val.astype(BF16).astype(F32)
-        block = att.at[core, pl.ds(i * height, height)]
-        copy = remote(block, block, g_send.at[i], g_recv.at[i], {'sp': partner})
-        copy.start()
-        g_copies.append(copy)
-    for i in range(blocks):
-        g_copies[i].wait_recv()
-    for g in range(2):
-        for j in range(group):
-            n = g * group + j
-            a_ref[:, n * HD:(n + 1) * HD] = att[g, pl.ds(j, seqs, stride=group), :].astype(BF16)
-    w_copy.wait()
-
-    chunks = part.shape[0]
-    wide = part.shape[2]
-
-    per_dot = 256 // wide
-
-    def compute(j):
-        val = jnp.dot(a_ref[...], w_buf[:, j * 256:(j + 1) * 256], preferred_element_type=F32)
-        for n in range(per_dot):
-            part[j * per_dot + n] = val[:, n * wide:(n + 1) * wide]
+        g_copy(i).start()
+
+    n_groups = 2
+    tall = seqs // n_groups
+    per_group = blocks // n_groups
+
+    def gather(g):
+        for i in range(per_group):
+            g_copy(g * per_group + i).wait_recv()
+        for side in range(2):
+            for j in range(group):
+                n = side * group + j
+                val = att[side, pl.ds(g * tall * group + j, tall, stride=group), :]
+                a_ref[g * tall:(g + 1) * tall, n * HD:(n + 1) * HD] = val.astype(BF16)
+
+    def guard(i, side, then):
+        if i % many < few:
+            then(i)
+        else:
+            @pl.when(side == 1)
+            def _():
+                then(i)
+
+    chunks = n_groups * many
+
+    def compute(i):
+        g, j = i // many, i % many
+        part[i] = jnp.dot(a_ref[g * tall:(g + 1) * tall, :], w_buf[:, j * wide:(j + 1) * wide], preferred_element_type=F32)
 
     def emit(half, side, i, ref):
-        at = (pl.ds(pl.multiple_of(half * seqs, seqs), seqs), pl.ds(pl.multiple_of(side * width + i * wide, wide), wide))
+        g, j = i // many, i % many
+        at = (pl.ds(pl.multiple_of(half * seqs + g * tall, tall), tall), pl.ds(pl.multiple_of((side * few + j) * wide, wide), wide))
         out_ref[at] = (h_ref[at].astype(F32) + ref[i]).astype(BF16)
 
     def e_copy(i):
@@ -391,61 +412,105 @@
         p2_copy(i).start()
         emit(1 - y, core, i, y_buf)
 
+    def add_end(i):
+        e_copy(i).wait_recv()
+        a_buf[i] = part[i] + e_buf[i]
+        b_copy(i).start()
+
+    def add_hub(i):
+        b_copy(i).wait_recv()
+        tot[i] = a_buf[i] + b_buf[i]
+        t_copy(i).start()
+        spread(i)
+
+    def take(i):
+        t_copy(i).wait_recv()
+        spread(i)
+
+    def send_end(i):
+        e_copy(i).start()
+
+    def at_core(i, then):
+        if 0 <= i < chunks:
+            guard(i, core, then)
+
+    settle(0)
+    settle(1)
+    settle(2)
+    gather(0)
+    on_side(core, lambda c, n: w_copy(c, n).wait())
+    early = 4
+
     @pl.when(is_hub)
     def _():
         lag, lag2 = 7, 15
-        for j in range(chunks // per_dot):
-            compute(j)
+        for i in range(early):
+            at_core(i, compute)
+        settle(3)
+        for i in range(early, few):
+            at_core(i, compute)
+
+        @pl.when(core == 1)
+        def _():
+            for i in range(few, many):
+                compute(i)
+
+        gather(1)
         for t in range(chunks + lag2):
-            if t < chunks:
-                e_copy(t).wait_recv()
-                a_buf[t] = part[t] + e_buf[t]
-                b_copy(t).start()
-            i = t - lag
-            if 0 <= i < chunks:
-                b_copy(i).wait_recv()
-                tot[i] = a_buf[i] + b_buf[i]
-                t_copy(i).start()
-                spread(i)
-            i = t - lag2
-            if 0 <= i < chunks:
-                pass_on(i)
+            if t < many:
+                at_core(t + many, compute)
+            at_core(t, add_end)
+            at_core(t - lag, add_hub)
+            at_core(t - lag2, pass_on)
         for i in range(chunks):
-            b_copy(i).wait_send()
-            t_copy(i).wait_send()
+            guard(i, core, lambda i: (b_copy(i).wait_send(), t_copy(i).wait_send()))
 
     @pl.when(jnp.logical_not(is_hub))
     def _():
         lag = 8
-        for j in range(chunks // per_dot + 1):
-            if j < chunks // per_dot:
-                compute(j)
-            for n in range(per_dot):
-                if j > 0:
-                    e_copy((j - 1) * per_dot + n).start()
+
+        def project(first_one, last_one):
+            for i in range(first_one, last_one + 1):
+                if i < last_one:
+                    compute(i)
+                if i > first_one:
+                    send_end(i - 1)
+
+        for g in range(n_groups):
+            if g == 0:
+                project(0, early)
+                settle(3)
+                project(early, few)
+            else:
+                gather(1)
+                project(many, many + few)
+
+            @pl.when(core == 1)
+            def _(g=g):
+                project(g * many + few, (g + 1) * many)
+
         for t in range(chunks + lag):
-            if t < chunks:
-                t_copy(t).wait_recv()
-                spread(t)
-            i = t - lag
-            if 0 <= i < chunks:
-                pass_on(i)
+            at_core(t, take)
+            at_core(t - lag, pass_on)
         for i in range(chunks):
-            e_copy(i).wait_send()
-
-    for i in range(chunks):
+            guard(i, core, lambda i: e_copy(i).wait_send())
+
+    def finish(i):
         p1_copy(i).wait_recv()
         emit(y, other, i, p1_buf)
         p2_copy(i).wait_recv()
         emit(1 - y, other, i, p2_buf)
+
     for i in range(chunks):
-        y_copy(i).wait_send()
-        p1_copy(i).wait_send()
-        p2_copy(i).wait_send()
+        guard(i, other, finish)
+    for i in range(chunks):
+        guard(i, core, lambda i: (y_copy(i).wait_send(), p1_copy(i).wait_send(), p2_copy(i).wait_send()))
     st_copy.wait_send()
     sy_copy.wait_send()
-    for copy in d_copies + y_copies + g_copies:
+    for copy in d_copies + y_copies:
         copy.wait_send()
+    for i in range(blocks):
+        g_copy(i).wait_send()
 
 
 def solution(mesh):
@@ -502,23 +567,24 @@
         )(positions, qkv, k_vmem, v_vmem)
         acc = acc.reshape(2, n_seq * group, head_dim)
 
-        width = d // 2
         depth = w_out.shape[0]
-        wide = CHUNK
-        chunks = width // wide
+        wide = 2 * CHUNK
+        few = d // wide * 13 // 32
+        many = d // wide - few
+        chunks = 2 * many
         blocks = 4
         seqs = n_seq // 2
-        slot = pltpu.VMEM((chunks, seqs, wide), F32)
+        slot = pltpu.VMEM((chunks, seqs // 2, wide), F32)
         whole = pltpu.VMEM((n_seq * group, head_dim), F32)
         half = pltpu.VMEM((seqs * group, head_dim), F32)
         tile = pltpu.VMEM((group, head_dim), F32)
         h_out = pl.pallas_call(
-            project_kernel,
+            functools.partial(project_kernel, (few, many)),
             out_shape=jax.ShapeDtypeStruct((n_seq, d), BF16),
             in_specs=[vmem, vmem, vmem, hbm],
             out_specs=vmem,
             scratch_shapes=[
-                pltpu.VMEM((depth, width), BF16), whole, tile, whole, tile, half, tile,
+                pltpu.VMEM((depth, many * wide), BF16), whole, tile, whole, tile, half, tile,
                 pltpu.VMEM((2, seqs * group, head_dim), F32), pltpu.VMEM((seqs, depth), BF16),
                 slot, slot, slot, slot, slot, slot, slot, slot,
                 dma(()), dma((2,)), dma((2,)), dma((2 * blocks,)), dma((2 * blocks,)), *[dma((blocks,)) for _ in range(4)],

time: 58.1 us -> 59.7 us (1.028)
  Pallas kernels: 56.3 us -> 57.8 us
    pallas_call x1, Pallas kernels: 37.1 us -> 38.7 us  [local_step(): pl.pallas_call(functools.partial(project_kernel, (few, many)), out_shape=...]
where the time goes in v5:
time: 59.7 us; the launch traced here: 59.5 us
  Pallas kernels  57.8 us (97%)
  local copies, waits for them, and re-layouts  0.98 us (2%)
  between operations  0.69 us (1%)
    pallas_call x1, Pallas kernels, local_step(): pl.pallas_call(functools.partial(project_kernel, (few, many)), out_shape=...  38.7 us
    pallas_call x1, Pallas kernels, local_step(): pl.pallas_call(qkv_kernel, out_shape=[pltpu.VMEM((4, share, n_seq, head_d...  12.5 us
    pallas_call x1, Pallas kernels, local_step(): pl.pallas_call(attention_kernel, out_shape=[jax.ShapeDtypeStruct(k_flat.s...  6.66 us

profile of v5, /device:TPU:0, one launch (start us, length us, event | category | flops | bytes accessed | tf_op | source)
XLA Modules:
  0.0 59.5 jit_solution(15103980414863281021)
XLA Ops:
  0.6 0.0 copy-start.1
  0.6 12.5 %qkv.1 = (f32[4,5,64,128]{3,2,1,0:T(8,128)S(1)}, bf16[64,512,128]{2,1,0:T(8,128)(2,1)S(1)}, bf16[64,512,128]{2,1,0:T(8,128)(2,1)S(1)}) custom-call(bf16[64,8192]{1,0:T(8,128)(2,1)} %h_ref.1, bf16[64,128]{1,0:T(8,128)(2,1)} %bitcast.13, s32[1,64]{1,0:T(1,128)} %bitcast.10, bf16[8192,2560]{1,0:T(8,128)(2,1)} %w_hbm.2, bf16[64,512,128]{2,1,0:T(8,128)(2,1)} %bitcast.11, ...), custom_call_target="tpu_custom_call" | custom-call | tf_op jit(solution)/shard_map/qkv/pallas_call | solution.py:537
  13.2 0.0 copy-done.1
  13.2 0.0 copy-start
  13.2 6.7 %attention.1 = (bf16[64,512,128]{2,1,0:T(8,128)(2,1)}, bf16[64,512,128]{2,1,0:T(8,128)(2,1)}, f32[2,64,8,128]{3,2,1,0:T(8,128)S(1)}, f32[2,8,128]{2,1,0:T(8,128)S(1)}) custom-call(s32[64]{0:T(128)S(1)} %copy-done.1, f32[20,64,128]{2,1,0:T(8,128)S(1)} %bitcast.8, bf16[64,512,128]{2,1,0:T(8,128)(2,1)S(1)} %get-tuple-element.11.k_ref, ...), custom_call_target="tpu_custom_call" | custom-call | tf_op jit(solution)/shard_map/attention/pallas_call | solution.py:553
  19.9 0.0 copy-done
  19.9 38.7 %project.1 = bf16[64,8192]{1,0:T(8,128)(2,1)S(1)} custom-call(bf16[64,8192]{1,0:T(8,128)(2,1)S(1)} %copy-done, f32[2,512,128]{2,1,0:T(8,128)S(1)} %bitcast.9, f32[2,8,128]{2,1,0:T(8,128)S(1)} %get-tuple-element.14.stat_ref, bf16[2048,8192]{1,0:T(8,128)(2,1)} %w_hbm.3), custom_call_target="tpu_custom_call" | custom-call | tf_op jit(solution)/shard_map/project/pallas_call | solution.py:581
  58.5 1.0 %copy.11 = bf16[64,8192]{1,0:T(8,128)(2,1)} copy(bf16[64,8192]{1,0:T(8,128)(2,1)S(1)} %project.1) | data formatting | bytes 2097152
Async XLA Ops:
  0.6 12.5 %copy-start.1 = (s32[64]{0:T(128)S(1)}, s32[64]{0:T(128)}, u32[]{:S(2)}) copy-start(s32[64]{0:T(128)} %pos_ref.1) | copy-start | bytes 772
  13.2 6.7 %copy-start = (bf16[64,8192]{1,0:T(8,128)(2,1)S(1)}, bf16[64,8192]{1,0:T(8,128)(2,1)}, u32[]{:S(2)}) copy-start(bf16[64,8192]{1,0:T(8,128)(2,1)} %h_ref.1) | copy-start | bytes 3145732

commit v6 on v3

--- a/solution.py
+++ b/solution.py
@@ -393,7 +393,7 @@
 
     @pl.when(is_hub)
     def _():
-        lag, lag2 = 7, 15
+        lag, lag2 = 12, 28
         for j in range(chunks // per_dot):
             compute(j)
         for t in range(chunks + lag2):
@@ -416,7 +416,7 @@
 
     @pl.when(jnp.logical_not(is_hub))
     def _():
-        lag = 8
+        lag = 18
         for j in range(chunks // per_dot + 1):
             if j < chunks // per_dot:
                 compute(j)

time: 58.1 us -> 58.2 us (level)
  no operation moved by 1% of the time
where the time goes in v6:
time: 58.2 us; the launch traced here: 58 us
  Pallas kernels  56.3 us (97%)
  local copies, waits for them, and re-layouts  0.98 us (2%)
  between operations  0.69 us (1%)
    pallas_call x1, Pallas kernels, local_step(): pl.pallas_call(project_kernel, out_shape=jax.ShapeDtypeStruct((n_seq, d),...  37.2 us
    pallas_call x1, Pallas kernels, local_step(): pl.pallas_call(qkv_kernel, out_shape=[pltpu.VMEM((4, share, n_seq, head_d...  12.5 us
    pallas_call x1, Pallas kernels, local_step(): pl.pallas_call(attention_kernel, out_shape=[jax.ShapeDtypeStruct(k_flat.s...  6.66 us

profile of v6, /device:TPU:0, one launch (start us, length us, event | category | flops | bytes accessed | tf_op | source)
XLA Modules:
  0.0 58.0 jit_solution(6797786532828864744)
XLA Ops:
  0.6 0.0 copy-start.1
  0.6 12.5 %qkv.1 = (f32[4,5,64,128]{3,2,1,0:T(8,128)S(1)}, bf16[64,512,128]{2,1,0:T(8,128)(2,1)S(1)}, bf16[64,512,128]{2,1,0:T(8,128)(2,1)S(1)}) custom-call(bf16[64,8192]{1,0:T(8,128)(2,1)} %h_ref.1, bf16[64,128]{1,0:T(8,128)(2,1)} %bitcast.13, s32[1,64]{1,0:T(1,128)} %bitcast.10, bf16[8192,2560]{1,0:T(8,128)(2,1)} %w_hbm.2, bf16[64,512,128]{2,1,0:T(8,128)(2,1)} %bitcast.11, ...), custom_call_target="tpu_custom_call" | custom-call | tf_op jit(solution)/shard_map/qkv/pallas_call | solution.py:472
  13.2 0.0 copy-done.1
  13.2 0.0 copy-start
  13.2 6.7 %attention.1 = (bf16[64,512,128]{2,1,0:T(8,128)(2,1)}, bf16[64,512,128]{2,1,0:T(8,128)(2,1)}, f32[2,64,8,128]{3,2,1,0:T(8,128)S(1)}, f32[2,8,128]{2,1,0:T(8,128)S(1)}) custom-call(s32[64]{0:T(128)S(1)} %copy-done.1, f32[20,64,128]{2,1,0:T(8,128)S(1)} %bitcast.8, bf16[64,512,128]{2,1,0:T(8,128)(2,1)S(1)} %get-tuple-element.11.k_ref, ...), custom_call_target="tpu_custom_call" | custom-call | tf_op jit(solution)/shard_map/attention/pallas_call | solution.py:488
  19.9 0.0 copy-done
  19.9 37.2 %project.1 = bf16[64,8192]{1,0:T(8,128)(2,1)S(1)} custom-call(bf16[64,8192]{1,0:T(8,128)(2,1)S(1)} %copy-done, f32[2,512,128]{2,1,0:T(8,128)S(1)} %bitcast.9, f32[2,8,128]{2,1,0:T(8,128)S(1)} %get-tuple-element.14.stat_ref, bf16[2048,8192]{1,0:T(8,128)(2,1)} %w_hbm.3), custom_call_target="tpu_custom_call" | custom-call | tf_op jit(solution)/shard_map/project/pallas_call | solution.py:515
  57.0 1.0 %copy.11 = bf16[64,8192]{1,0:T(8,128)(2,1)} copy(bf16[64,8192]{1,0:T(8,128)(2,1)S(1)} %project.1) | data formatting | bytes 2097152
Async XLA Ops:
  0.6 12.5 %copy-start.1 = (s32[64]{0:T(128)S(1)}, s32[64]{0:T(128)}, u32[]{:S(2)}) copy-start(s32[64]{0:T(128)} %pos_ref.1) | copy-start | bytes 772
  13.2 6.7 %copy-start = (bf16[64,8192]{1,0:T(8,128)(2,1)S(1)}, bf16[64,8192]{1,0:T(8,128)(2,1)}, u32[]{:S(2)}) copy-start(bf16[64,8192]{1,0:T(8,128)(2,1)} %h_ref.1) | copy-start | bytes 3145732

commit v7 on v6

--- a/solution.py
+++ b/solution.py
@@ -393,7 +393,7 @@
 
     @pl.when(is_hub)
     def _():
-        lag, lag2 = 12, 28
+        lag, lag2 = 4, 10
         for j in range(chunks // per_dot):
             compute(j)
         for t in range(chunks + lag2):
@@ -416,7 +416,7 @@
 
     @pl.when(jnp.logical_not(is_hub))
     def _():
-        lag = 18
+        lag = 6
         for j in range(chunks // per_dot + 1):
             if j < chunks // per_dot:
                 compute(j)
@@ -504,7 +504,7 @@
 
         width = d // 2
         depth = w_out.shape[0]
-        wide = CHUNK
+        wide = 2 * CHUNK
         chunks = width // wide
         blocks = 4
         seqs = n_seq // 2

time: 58.2 us -> 56.6 us (0.973)
  Pallas kernels: 56.3 us -> 54.7 us
    pallas_call x1, Pallas kernels: 37.2 us -> 35.6 us  [local_step(): pl.pallas_call(project_kernel, out_shape=jax.ShapeDtypeStruct((n_seq, d),...]
where the time goes in v7:
time: 56.6 us; the launch traced here: 56.4 us
  Pallas kernels  54.7 us (97%)
  local copies, waits for them, and re-layouts  0.98 us (2%)
  between operations  0.69 us (1%)
    pallas_call x1, Pallas kernels, local_step(): pl.pallas_call(project_kernel, out_shape=jax.ShapeDtypeStruct((n_seq, d),...  35.6 us
    pallas_call x1, Pallas kernels, local_step(): pl.pallas_call(qkv_kernel, out_shape=[pltpu.VMEM((4, share, n_seq, head_d...  12.5 us
    pallas_call x1, Pallas kernels, local_step(): pl.pallas_call(attention_kernel, out_shape=[jax.ShapeDtypeStruct(k_flat.s...  6.66 us

profile of v7, /device:TPU:0, one launch (start us, length us, event | category | flops | bytes accessed | tf_op | source)
XLA Modules:
  0.0 56.4 jit_solution(3472375899514939081)
XLA Ops:
  0.6 0.0 copy-start.1
  0.6 12.5 %qkv.1 = (f32[4,5,64,128]{3,2,1,0:T(8,128)S(1)}, bf16[64,512,128]{2,1,0:T(8,128)(2,1)S(1)}, bf16[64,512,128]{2,1,0:T(8,128)(2,1)S(1)}) custom-call(bf16[64,8192]{1,0:T(8,128)(2,1)} %h_ref.1, bf16[64,128]{1,0:T(8,128)(2,1)} %bitcast.13, s32[1,64]{1,0:T(1,128)} %bitcast.10, bf16[8192,2560]{1,0:T(8,128)(2,1)} %w_hbm.2, bf16[64,512,128]{2,1,0:T(8,128)(2,1)} %bitcast.11, ...), custom_call_target="tpu_custom_call" | custom-call | tf_op jit(solution)/shard_map/qkv/pallas_call | solution.py:472
  13.2 0.0 copy-done.1
  13.2 0.0 copy-start
  13.2 6.7 %attention.1 = (bf16[64,512,128]{2,1,0:T(8,128)(2,1)}, bf16[64,512,128]{2,1,0:T(8,128)(2,1)}, f32[2,64,8,128]{3,2,1,0:T(8,128)S(1)}, f32[2,8,128]{2,1,0:T(8,128)S(1)}) custom-call(s32[64]{0:T(128)S(1)} %copy-done.1, f32[20,64,128]{2,1,0:T(8,128)S(1)} %bitcast.8, bf16[64,512,128]{2,1,0:T(8,128)(2,1)S(1)} %get-tuple-element.11.k_ref, ...), custom_call_target="tpu_custom_call" | custom-call | tf_op jit(solution)/shard_map/attention/pallas_call | solution.py:488
  19.9 0.0 copy-done
  19.9 35.6 %project.1 = bf16[64,8192]{1,0:T(8,128)(2,1)S(1)} custom-call(bf16[64,8192]{1,0:T(8,128)(2,1)S(1)} %copy-done, f32[2,512,128]{2,1,0:T(8,128)S(1)} %bitcast.9, f32[2,8,128]{2,1,0:T(8,128)S(1)} %get-tuple-element.14.stat_ref, bf16[2048,8192]{1,0:T(8,128)(2,1)} %w_hbm.3), custom_call_target="tpu_custom_call" | custom-call | tf_op jit(solution)/shard_map/project/pallas_call | solution.py:515
  55.4 1.0 %copy.11 = bf16[64,8192]{1,0:T(8,128)(2,1)} copy(bf16[64,8192]{1,0:T(8,128)(2,1)S(1)} %project.1) | data formatting | bytes 2097152
Async XLA Ops:
  0.6 12.5 %copy-start.1 = (s32[64]{0:T(128)S(1)}, s32[64]{0:T(128)}, u32[]{:S(2)}) copy-start(s32[64]{0:T(128)} %pos_ref.1) | copy-start | bytes 772
  13.2 6.7 %copy-start = (bf16[64,8192]{1,0:T(8,128)(2,1)S(1)}, bf16[64,8192]{1,0:T(8,128)(2,1)}, u32[]{:S(2)}) copy-start(bf16[64,8192]{1,0:T(8,128)(2,1)} %h_ref.1) | copy-start | bytes 3145732
